TPU v7x, 32 devices: a whole 2x2x4 slice. The times are simulated.
32 devices in a mesh: gx: 8 (over y, x, core), gy: 4 (over z).
Axes of the slice: x: 2, y: 2, z: 4, core: 2. Of those that a mesh axis runs over, the one named last changes fastest.
Arguments:
- right_side: float32 [3, 128, 32, 256], P(None, 'gx', 'gy'), may hold values from -12 to 12
- labels: int32 [128, 32, 256], P('gx', 'gy'), may hold values 0 or 1
Outputs:
- solution: float32 [3, 128, 32, 256], P(None, 'gx', 'gy')
- residual: float32 [3, 128, 32, 256], P(None, 'gx', 'gy')
All inputs are finite; a program needn't handle non-finite values. No bound on the sum of `labels` on one device may be relied on, other than what follows from the above.
Results may differ from a plain program's by a relative error of at most 0.0003.
Values sent between devices are 32-bit elements; how exact they have to be, the bound alone decides.
No kernel may reach another device: no remote copies, remote signals or barrier semaphores. Data moves between devices by JAX's collectives and lax.ppermute only.
A program may use at most 64 MiB of HBM per device.

v0:
```python
import jax
import jax.numpy as jnp
from jax import lax
from jax.experimental import pallas as pl
from jax.experimental.pallas import tpu as pltpu
from jax.sharding import PartitionSpec as P


ITERS = 4
HALO = ITERS
LAMBDA_SOFT = 0.5769231
LAMBDA_RISE = 1.6452991
SHEAR_SOFT = 0.3846154
SHEAR_RISE = 2.9487179
KAPPA = 0.05
SHIFT = (0.25, 1.6, 1.5, 1.5)
STEP = (1.0, 0.6, 0.6, 0.6)
SUMS = 14
WIDTH = 4


def shifted(shard, axis, by):
    size = lax.axis_size(axis)
    return lax.ppermute(shard, axis, [(i, (i + by) % size) for i in range(size)])


def roll(v, by, axis):
    return pltpu.roll(v, by % v.shape[axis], axis)


def get(ref, *index, row=0, rows=None):
    rows = ref.shape[-2] - 8 if rows is None else rows
    parts = [ref[(*index, i, slice(row, row + rows))] for i in range(ref.shape[-3])]
    return jnp.concatenate(parts, 1)


def put(ref, *index, value):
    rows = value.shape[0]
    for i in range(ref.shape[-3]):
        part = value[:, 128 * i : 128 * (i + 1)]
        ref[(*index, i, slice(0, rows))] = part
        ref[(*index, i, slice(rows, rows + 8))] = part[:8]


def gather_modes(v, up, ahead, ahead_up):
    near = (v + up, up - v)
    far = (ahead + ahead_up, ahead_up - ahead)
    out = {}
    for by in (0, 1):
        out[by, 0] = near[by] + far[by]
        out[by, 1] = far[by] - near[by]
    return out


def scatter_modes(r, below):
    part = []
    for bz in (0, 1):
        part.append((r[0, bz] - r[1, bz]) + (below[0, bz] + below[1, bz]))
    return part[0] - part[1], part[0] + part[1]


def voxel_forces(c, stiff):
    lam = (LAMBDA_SOFT / 16) + (LAMBDA_RISE / 16) * stiff
    mu = (SHEAR_SOFT / 16) + (SHEAR_RISE / 16) * stiff
    mu2 = mu + mu
    lam3 = lam * (1.0 / 3)
    mu3 = mu * (1.0 / 3)
    top = ((LAMBDA_SOFT + 4 * SHEAR_SOFT) / 144) + ((LAMBDA_RISE + 4 * SHEAR_RISE) / 144) * stiff
    f = {}
    normal = ((0, 1, 0, 0), (1, 0, 1, 0), (2, 0, 0, 1))
    t = lam * (c[normal[0]] + c[normal[1]] + c[normal[2]])
    for p in normal:
        f[p] = t + mu2 * c[p]
    for p, q in (
        ((0, 1, 1, 0), (2, 0, 1, 1)),
        ((0, 1, 0, 1), (1, 0, 1, 1)),
        ((1, 1, 1, 0), (2, 1, 0, 1)),
    ):
        t = lam3 * (c[p] + c[q])
        f[p] = t + mu * c[p]
        f[q] = t + mu * c[q]
    for comp in range(3):
        p = (comp, 1, 1, 1)
        f[p] = top * c[p]
    for p, q in (
        ((0, 0, 1, 0), (1, 1, 0, 0)),
        ((0, 0, 0, 1), (2, 1, 0, 0)),
        ((1, 0, 0, 1), (2, 0, 1, 0)),
    ):
        f[p] = f[q] = mu * (c[p] + c[q])
    bend = ((0, 0, 1, 1), (1, 1, 0, 1), (2, 1, 1, 0))
    t = c[bend[0]] + c[bend[1]] + c[bend[2]]
    for p in bend:
        f[p] = mu3 * (t + c[p])
    return f


MODES = [(comp, by, bz) for comp in range(3) for by in (0, 1) for bz in (0, 1)]


def strides(start, stop, width, body, carry):
    def several(i, carry):
        return body(start + width * i, carry)

    return lax.fori_loop(0, -((start - stop) // width), several, carry)


def pairs(start, stop, body, carry):
    return strides(start, stop, 2, lambda n, c: body(n + 1, body(n, c)), carry)


def tiles_of(rows, depth):
    return [(slice(a, a + 8), slice(b, b + 128)) for a in range(0, rows, 8) for b in range(0, depth, 128)]


def diagonal_layer(cells, turned, edge, first_row):
    lz = cells + turned
    row_id = lax.broadcasted_iota(jnp.int32, lz.shape, 0)
    return lz + jnp.where(row_id == first_row, jnp.broadcast_to(edge, lz.shape), roll(lz, 1, 0))


def diagonal_from(two_layers):
    base = 8 * (LAMBDA_SOFT + 4 * SHEAR_SOFT) / 9 + KAPPA
    return base + ((LAMBDA_RISE + 4 * SHEAR_RISE) / 9) * two_layers


def forward_planes(first, last, node_ref, turn_ref, q_ref):
    rows = node_ref.shape[-2] - 8
    tiles = tiles_of(rows, 128 * node_ref.shape[-3])
    for n in range(first, last):
        for comp in range(3):
            put(turn_ref, comp, n, value=roll(get(node_ref, comp, n), -1, 1))

    def forward(n, _):
        for comp in range(3):
            out = gather_modes(
                get(node_ref, comp, n),
                get(node_ref, comp, n, row=1, rows=rows),
                get(turn_ref, comp, n),
                get(turn_ref, comp, n, row=1, rows=rows),
            )
            for i, (cc, by, bz) in enumerate(MODES):
                if cc == comp:
                    for j, tile in enumerate(tiles):
                        q_ref[n, i, j] = out[by, bz][tile]
        return _

    pairs(first, last, forward, 0)


def voxel_layers(j, first, last, cells_at, q_ref, f_ref):
    across, tall = f_ref.shape[-3], f_ref.shape[-2]
    line, lanes = divmod(j, across)
    row = 8 * (line + 1)

    def store(n, i, value):
        f_ref[n, i, lanes, row : row + 8] = value
        if row + 8 == tall:
            f_ref[n, i, lanes, 0:8] = value

    def voxels(n, carry):
        near, behind = carry
        far = [q_ref[n + 1, i, j] for i in range(len(MODES))]
        c = {}
        for i, (comp, by, bz) in enumerate(MODES):
            if (by, bz) != (0, 0):
                c[comp, 0, by, bz] = near[i] + far[i]
            c[comp, 1, by, bz] = far[i] - near[i]
        f = voxel_forces(c, cells_at(n))
        ahead = []
        for i, (comp, by, bz) in enumerate(MODES):
            up = f[comp, 1, by, bz]
            if (by, bz) != (0, 0):
                flat = f[comp, 0, by, bz]
                store(n, i, behind[i] + (flat - up))
                ahead.append(flat + up)
            else:
                store(n, i, behind[i] - up)
                ahead.append(up)
        return far, ahead

    near = [q_ref[first, i, j] for i in range(len(MODES))]
    pairs(first, last, voxels, (near, [jnp.zeros_like(v) for v in near]))


def collect(n, f_ref, image_ref):
    rows = f_ref.shape[-2] - 8
    for comp in range(3):
        here, below = {}, {}
        for i, (cc, by, bz) in enumerate(MODES):
            if cc == comp:
                here[by, bz] = get(f_ref, n, i, row=8, rows=rows)
                below[by, bz] = get(f_ref, n, i, row=7, rows=rows)
        kept, moved = scatter_modes(here, below)
        image_ref[comp, n] = kept + roll(moved, 1, 1)


def update(k, inv):
    gain = inv * (1 / STEP[k])
    own = KAPPA * gain - SHIFT[k] / STEP[k]

    def new(force, t, older):
        out = force * gain + t * own
        return out - (STEP[k - 1] / STEP[k]) * older() if k > 1 else out

    return new


def packed_sums(totals):
    lane = lax.broadcasted_iota(jnp.int32, (1, 128), 1)
    packed = jnp.zeros((1, 128), jnp.float32)
    for i, v in enumerate(totals):
        s = jnp.sum(jnp.sum(v, axis=0, keepdims=True), axis=1, keepdims=True)
        packed = jnp.where(lane == i, s, packed)
    return packed


def y_parts(own_x):
    h = HALO
    mid = own_x - 2 * h

    def node(comp, x):
        if x < h:
            return 0, 4 * h + 1 + comp * h + x
        if x >= own_x - h:
            return 0, comp * h + x - (own_x - h)
        return 1, comp * mid + x - h

    def cell(x):
        if x < h:
            return 0, 7 * h + 1 + x
        if x >= own_x - h - 1:
            return 0, 3 * h + x - (own_x - h - 1)
        return 1, 3 * mid + x - h

    def edge(x):
        if x < h:
            return 0, h + 1 + x
        if x >= own_x - h - 1:
            return 0, x - (own_x - h - 1)
        return 1, x - h

    blocks = (8 * h + 1, 4 * mid - 1)
    edge_blocks = (-(-(2 * h + 1) // h), -(-(mid - 1) // h))
    return node, cell, edge, blocks, edge_blocks


def inside_kernel(
    r_own, lab_own, side_a, side_b, edge_a, edge_b,
    t_out, d_out, inv_out, edge_out, sums_out,
    side_ref, edge_ref, t_ref, turn_ref, image_ref, q_ref, f_ref,
):
    own_x, own_y, depth = r_own.shape[1:]
    rows = own_y + side_ref.shape[2]
    tiles = tiles_of(rows, depth)
    count = own_x - 1

    def both(block, side):
        return jnp.concatenate([block, side], 0)

    node_at, cell_at, edge_at = y_parts(own_x)[:3]
    sides, edges = (side_a, side_b), (edge_a, edge_b)
    for x in range(own_x):
        for comp in range(3):
            part, place = node_at(comp, x)
            side_ref[comp, x] = sides[part][place]
        part, place = cell_at(x)
        side_ref[3, x] = sides[part][place]
        part, place = edge_at(x)
        edge_ref[x : x + 1] = edges[part][place : place + 1]
    lines = edge_ref[...]
    edge_ref[...] = lines + roll(lines, 1, 1)
    for m in range(own_x):
        put(turn_ref, 0, m, value=roll(both(lab_own[m], side_ref[3, m]), 1, 1))

    def layer(m):
        cells = both(lab_own[m], side_ref[3, m])
        return diagonal_layer(cells, get(turn_ref, 0, m), edge_ref[pl.ds(m, 1), :], own_y + HALO)

    def start(p, before):
        here = layer(p + 1)
        diag = diagonal_from(before + here)
        inv = 1.0 / diag
        inv_out[p + 1] = inv
        d_out[p + 1] = diag[:own_y]
        for comp in range(3):
            t = both(r_own[comp, p + 1], side_ref[comp, p + 1]) * inv
            put(t_ref, 0, comp, p, value=t)
            t_out[0, comp, p + 1] = t[:own_y]
        return here

    before = pairs(0, count - 1, start, layer(0))
    start(count - 1, before)

    totals = []
    for k in range(ITERS):
        first, last = k, count - k
        for i, p in enumerate((first, first + 1, last - 2, last - 1)):
            for comp in range(3):
                edge_out[k, comp, i] = get(t_ref, k, comp, p)
        forward_planes(first, last, t_ref.at[k], turn_ref, q_ref)
        for j, (line, lanes) in enumerate(tiles):

            def cells_at(n):
                if line.start < own_y:
                    return lab_own[n + 1, line, lanes]
                return side_ref[3, n + 1, line.start - own_y : line.stop - own_y, lanes]

            voxel_layers(j, first, last - 1, cells_at, q_ref, f_ref)

        def advance(p, acc):
            acc = list(acc)
            new = update(k, inv_out[p + 1])
            for comp in range(3):
                t = get(t_ref, k, comp, p)
                force = image_ref[comp, p]
                image = force[:own_y] + KAPPA * t[:own_y]
                for j in range(k + 1):
                    acc[j] += get(t_ref, j, comp, p, rows=own_y) * image
                acc[k + 1] += t[:own_y] * r_own[comp, p + 1]
                t = new(force, t, lambda: get(t_ref, k - 1, comp, p))
                if k + 1 < ITERS:
                    put(t_ref, k + 1, comp, p, value=t)
                t_out[k + 1, comp, p + 1] = t[:own_y]
            return tuple(acc)

        def several(n, acc):
            for u in range(WIDTH):
                acc = advance(n + u, acc)
            for u in range(WIDTH):
                collect(n + WIDTH + u, f_ref, image_ref)
            return acc

        begin, end = first + 1, last - 1
        whole = begin + (end - begin) // WIDTH * WIDTH
        for p in range(begin, begin + WIDTH):
            collect(p, f_ref, image_ref)
        acc = (jnp.zeros((own_y, depth), jnp.float32),) * (k + 2)
        acc = strides(begin, whole, WIDTH, several, acc)
        for p in range(whole, end):
            acc = advance(p, acc)
        totals.extend(acc)
    sums_out[...] = packed_sums(totals)


def finish_kernel(
    r_own, lab_own, side_a, side_b, edge_a, below, above, below_side, above_side,
    t_in, inv_in, edge_in, sums_in,
    t_out, d_out, sums_out,
    cell_ref, inv_ref, u_ref, turn_ref, image_ref, q_ref, f_ref,
):
    h = HALO
    own_x, own_y, depth = r_own.shape[1:]
    rows = own_y + side_a.shape[1]
    tiles = tiles_of(rows, depth)
    left, right = h + 3, h + 2
    node_at, cell_at, edge_at = y_parts(own_x)[:3]
    sides = (side_a, side_b)

    def nodes(comp, x):
        if x < 0:
            return jnp.concatenate([below[comp * h + h + x], below_side[comp * h + h + x]], 0)
        if x >= own_x:
            i = comp * h + x - own_x
            return jnp.concatenate([above[i], above_side[i]], 0)
        part, place = node_at(comp, x)
        return jnp.concatenate([r_own[comp, x], sides[part][place]], 0)

    def cells(x):
        if x < 0:
            i = 3 * h + h + 1 + x
            return jnp.concatenate([below[i], below_side[i]], 0)
        if x >= own_x:
            i = 3 * h + x - own_x
            return jnp.concatenate([above[i], above_side[i]], 0)
        part, place = cell_at(x)
        return jnp.concatenate([lab_own[x], sides[part][place]], 0)

    def edge(x):
        if x < 0:
            return below_side[4 * h + 1, h + 1 + x : h + 2 + x]
        if x >= own_x:
            return above_side[4 * h, x - own_x : x - own_x + 1]
        place = edge_at(x)[1]
        return edge_a[place : place + 1]

    for x in [*range(-h - 1, ITERS + 1), *range(own_x - 1 - ITERS, own_x + h)]:
        cell_ref[x + h + 1] = cells(x)

    def layer(x):
        e = edge(x)
        c = cell_ref[x + h + 1]
        return diagonal_layer(c, roll(c, 1, 1), e + roll(e, 1, 1), own_y + h)

    def place(k, x):
        return x - (k - h) if x < own_x // 2 else left + x - (own_x - 2 - k)

    for start, stop in ((-h, 1), (own_x, own_x + h)):
        layers = [layer(x) for x in range(start - 1, stop)]
        for x in range(start, stop):
            diag = diagonal_from(layers[x - start] + layers[x - start + 1])
            inv = 1.0 / diag
            inv_ref[x + h] = inv
            if x == 0:
                d_out[...] = diag[:own_y]
            for comp in range(3):
                t = nodes(comp, x) * inv
                put(u_ref, 0, comp, place(0, x), value=t)
                if x == 0:
                    t_out[0, comp, 0] = t[:own_y]
    for x in [*range(1, ITERS + 1), *range(own_x - ITERS, own_x)]:
        inv_ref[x + h] = inv_in[x]

    def own_rows(j, comp, x):
        ref = t_out if x <= j or x >= own_x - j else t_in
        return ref[j, comp, x]

    totals = []
    for k in range(ITERS):
        for comp in range(3):
            for i, p in enumerate((left - 2, left - 1, left, left + 1)):
                put(u_ref, k, comp, p, value=edge_in[k, comp, i])
        forward_planes(0, left + right, u_ref.at[k], turn_ref, q_ref)
        for j, (line, lanes) in enumerate(tiles):
            voxel_layers(j, 0, left - 1, lambda n: cell_ref[n + k + 1, line, lanes], q_ref, f_ref)
            shift = own_x - 2 - k - left + h + 1
            voxel_layers(
                j, left, left + right - 1, lambda n: cell_ref[n + shift, line, lanes], q_ref, f_ref
            )
        planes = [*range(k - h + 1, k + 2), *range(own_x - 1 - k, own_x + h - 1 - k)]
        if k + 1 == ITERS:
            planes = [x for x in planes if 0 <= x < own_x]
        for x in planes:
            collect(place(k, x), f_ref, image_ref)
        acc = [jnp.zeros((own_y, depth), jnp.float32)] * (k + 2)
        for x in planes:
            new = update(k, inv_ref[x + h])
            own = 0 <= x < own_x
            for comp in range(3):
                t = get(u_ref, k, comp, place(k, x))
                force = image_ref[comp, place(k, x)]
                if own:
                    image = force[:own_y] + KAPPA * t[:own_y]
                    for j in range(k + 1):
                        acc[j] += own_rows(j, comp, x) * image
                    acc[k + 1] += t[:own_y] * r_own[comp, x]
                t = new(force, t, lambda: get(u_ref, k - 1, comp, place(k - 1, x)))
                if k + 1 < ITERS:
                    put(u_ref, k + 1, comp, place(k + 1, x), value=t)
                if own:
                    t_out[k + 1, comp, x] = t[:own_y]
        totals.extend(acc)
    sums_out[...] = jnp.broadcast_to((packed_sums(totals) + sums_in[...])[None], sums_out.shape)


def pack_kernel(
    r_hbm, lab_hbm, r_out, lab_out, up_a, down_a, up_b, down_b, next_out, previous_out, lab_in, arrived
):
    h = HALO
    own_x, own_y = lab_in.shape[:2]
    copies = [
        pltpu.make_async_copy(r_hbm, r_out, arrived.at[0]),
        pltpu.make_async_copy(lab_hbm, lab_in, arrived.at[1]),
    ]
    for copy in copies:
        copy.start()
    for copy in copies:
        copy.wait()

    ups, downs = (up_a, up_b), (down_a, down_b)
    node_at, cell_at, edge_at, blocks, _ = y_parts(own_x)
    for x in range(own_x):
        l = lab_in[x].astype(jnp.float32)
        lab_out[x] = l
        part, place = cell_at(x)
        ups[part][place] = l[own_y - h :]
        downs[part][place] = l[:h]
        part, place = edge_at(x)
        ups[part][blocks[part] + place // h, place % h : place % h + 1] = l[own_y - h - 1 : own_y - h]
        if x < h:
            previous_out[3 * h + x] = l
        if x >= own_x - h - 1:
            next_out[3 * h + x - (own_x - h - 1)] = l
        for comp in range(3):
            r = r_out[comp, x]
            part, place = node_at(comp, x)
            ups[part][place] = r[own_y - h :]
            downs[part][place] = r[:h]
            if x < h:
                previous_out[comp * h + x] = r
            if x >= own_x - h:
                next_out[comp * h + x - (own_x - h)] = r


def combine_kernel(sums_ref, inner_ref, outer_ref, d_inner, d_outer, x_out, r_out):
    total = jnp.sum(sums_ref[...], axis=0, keepdims=True)
    lane = lax.broadcasted_iota(jnp.int32, total.shape, 1)
    entry = [
        jnp.sum(jnp.where(lane == i, total, 0.0), axis=1, keepdims=True) for i in range(SUMS)
    ]
    gram, right = {}, []
    place = 0
    for k in range(ITERS):
        for j in range(k + 1):
            gram[j, k] = gram[k, j] = entry[place]
            place += 1
        right.append(entry[place])
        place += 1
    scale = [gram[k, k] for k in range(ITERS)]
    inv, low = [], {}
    for k in range(ITERS):
        pivot = gram[k, k]
        good = pivot > 1e-7 * scale[k]
        inv.append(jnp.where(good, 1.0 / jnp.where(good, pivot, 1.0), 0.0))
        for i in range(k + 1, ITERS):
            low[i, k] = gram[i, k] * inv[k]
        for i in range(k + 1, ITERS):
            for j in range(k + 1, i + 1):
                gram[i, j] = gram[j, i] = gram[i, j] - low[i, k] * gram[j, k]
            right[i] = right[i] - low[i, k] * right[k]
    y = [None] * ITERS
    for k in reversed(range(ITERS)):
        y[k] = right[k] * inv[k]
        for i in range(k + 1, ITERS):
            y[k] = y[k] - low[i, k] * y[i]
    e = [jnp.ones_like(y[0])] + [jnp.zeros_like(y[0]) for _ in range(ITERS)]
    for k in range(ITERS):
        e[k + 1] = e[k + 1] - STEP[k] * y[k]
        e[k] = e[k] - SHIFT[k] * y[k]
        if k > 1:
            e[k - 1] = e[k - 1] - STEP[k - 1] * y[k]
    y = [jnp.broadcast_to(v, d_outer.shape) for v in y]
    e = [jnp.broadcast_to(v, d_outer.shape) for v in e]

    own_x = d_inner.shape[0]

    def plane(n, outer):
        diag = d_inner[n] if outer is None or n > 0 else d_outer[...]
        for comp in range(3):
            t = []
            for k in range(ITERS + 1):
                edge = outer is not None and (n <= k or n >= own_x - k)
                t.append((outer_ref if edge else inner_ref)[k, comp, n])
            x, r = y[0] * t[0], e[0] * t[0]
            for k in range(1, ITERS):
                x = x + y[k] * t[k]
                r = r + e[k] * t[k]
            r = r + e[ITERS] * t[ITERS]
            x_out[comp, n] = x
            r_out[comp, n] = r * diag

    for n in [*range(ITERS + 1), *range(own_x - ITERS, own_x)]:
        plane(n, True)

    def body(n, _):
        plane(n, None)
        return _

    lax.fori_loop(ITERS + 1, own_x - ITERS, body, 0)


def local(right_side, labels):
    own_x, own_y, depth = labels.shape
    h = HALO
    f32 = jnp.float32
    devices = lax.axis_size("gx") * lax.axis_size("gy")
    small = pltpu.CompilerParams(vmem_limit_bytes=16 * 2**20)
    blocks, edge_blocks = y_parts(own_x)[3:]
    right_side, lab, up_a, down_a, up_b, down_b, to_next, to_previous = pl.pallas_call(
        pack_kernel,
        out_shape=(
            jax.ShapeDtypeStruct(right_side.shape, f32),
            jax.ShapeDtypeStruct(labels.shape, f32),
            jax.ShapeDtypeStruct((blocks[0] + edge_blocks[0], h, depth), f32),
            jax.ShapeDtypeStruct((blocks[0], h, depth), f32),
            jax.ShapeDtypeStruct((blocks[1] + edge_blocks[1], h, depth), f32),
            jax.ShapeDtypeStruct((blocks[1], h, depth), f32),
            jax.ShapeDtypeStruct((4 * h + 1, own_y, depth), f32),
            jax.ShapeDtypeStruct((4 * h, own_y, depth), f32),
        ),
        in_specs=[pl.BlockSpec(memory_space=pltpu.HBM)] * 2,
        scratch_shapes=[pltpu.VMEM(labels.shape, jnp.int32), pltpu.SemaphoreType.DMA((2,))],
        compiler_params=small,
        name="pack",
    )(*(pltpu.with_memory_space_constraint(v, pltpu.HBM) for v in (right_side, labels)))

    minus_a, plus_a = shifted(up_a, "gy", 1), shifted(down_a, "gy", -1)
    minus_b, plus_b = shifted(up_b, "gy", 1), shifted(down_b, "gy", -1)
    below = shifted(to_next, "gx", 1)
    above = shifted(to_previous, "gx", -1)
    minus_a, plus_a, below, above = lax.optimization_barrier((minus_a, plus_a, below, above))

    def stack(minus, plus, count):
        side = jnp.concatenate([plus[:count], minus[:count]], 1)
        return side, minus[count:].reshape(-1, depth)

    def corner(block, rows):
        rows = jnp.pad(rows, ((0, 2 * h - rows.shape[0]), (0, 0)))
        return jnp.concatenate([block, rows[None]], 0)

    side_a, edge_a = stack(minus_a, plus_a, blocks[0])
    below_side = shifted(corner(side_a[: 4 * h + 1], edge_a[: h + 1]), "gx", 1)
    last = corner(side_a[4 * h + 1 :], edge_a[h + 1 : 2 * h + 1])
    above_side = shifted(last, "gx", -1)
    side_b, edge_b = stack(minus_b, plus_b, blocks[1])

    rows = own_y + 2 * h
    tiles = (rows // 8) * (depth // 128)

    across = depth // 128

    def kept(*lead):
        return pltpu.VMEM((*lead, across, rows + 8, 128), f32)

    def scratch(planes):
        return [
            kept(ITERS, 3, planes),
            kept(3, planes),
            pltpu.VMEM((3, planes, rows, depth), f32),
            pltpu.VMEM((planes, len(MODES), tiles + 1, 8, 128), f32),
            kept(planes, len(MODES)),
        ]

    planes = own_x + 2 * WIDTH
    own_basis = jax.ShapeDtypeStruct((ITERS + 1, 3, own_x, own_y, depth), f32)
    inner, d_inner, inverse, borders, inner_sums = pl.pallas_call(
        inside_kernel,
        out_shape=(
            own_basis,
            jax.ShapeDtypeStruct((own_x, own_y, depth), f32),
            jax.ShapeDtypeStruct((own_x, rows, depth), f32),
            jax.ShapeDtypeStruct((ITERS, 3, 4, rows, depth), f32),
            jax.ShapeDtypeStruct((1, 128), f32),
        ),
        scratch_shapes=[
            pltpu.VMEM((4, own_x, 2 * h, depth), f32),
            pltpu.VMEM((own_x, depth), f32),
            *scratch(planes),
        ],
        compiler_params=pltpu.CompilerParams(vmem_limit_bytes=28 * 2**20),
        name="inside",
    )(right_side, lab, side_a, side_b, edge_a, edge_b)

    strips = 4 * h + 12
    outer, d_outer, sums = pl.pallas_call(
        finish_kernel,
        out_shape=(
            own_basis,
            jax.ShapeDtypeStruct((own_y, depth), f32),
            jax.ShapeDtypeStruct((devices, 1, 128), f32),
        ),
        scratch_shapes=[
            pltpu.VMEM((own_x + 2 * h + 2, rows, depth), f32),
            pltpu.VMEM((own_x + 2 * h, rows, depth), f32),
            *scratch(strips),
        ],
        compiler_params=pltpu.CompilerParams(vmem_limit_bytes=28 * 2**20),
        name="finish",
    )(
        right_side, lab, side_a, side_b, edge_a, below, above, below_side, above_side,
        inner, inverse, borders, inner_sums,
    )

    everyone = lax.all_to_all(sums, ("gx", "gy"), 0, 0)
    out = jax.ShapeDtypeStruct(right_side.shape, f32)
    return pl.pallas_call(combine_kernel, out_shape=(out, out), compiler_params=small, name="combine")(
        everyone.reshape(devices, 128), inner, outer, d_inner, d_outer
    )


def solution(mesh):
    in_specs = (P(None, "gx", "gy", None), P("gx", "gy", None))
    out_specs = (P(None, "gx", "gy", None), P(None, "gx", "gy", None))
    return jax.shard_map(local, mesh=mesh, in_specs=in_specs, out_specs=out_specs, check_vma=False)
```

profile of v0, /device:TPU:0, one launch (start us, length us, event | category | flops | bytes accessed | tf_op | source)
XLA Modules:
  0.0 49.4 jit_solution(18334188742282187170)
XLA Ops:
  0.6 1.1 %pack.1 = (f32[3,16,8,256]{3,2,1,0:T(8,128)S(1)}, f32[16,8,256]{2,1,0:T(8,128)S(1)}, f32[36,4,256]{2,1,0:T(4,128)S(1)}, f32[33,4,256]{2,1,0:T(4,128)S(1)}, f32[3...) custom-call(f32[3,16,8,256]{3,2,1,0:T(8,128)} %r_hbm.1, ...), custom_call_target="tpu_custom_call" | custom-call | tf_op jit(solution)/shard_map/pack/pallas_call | solution.py:569
  1.8 3.1 %collective-permute-start = (f32[36,4,256]{2,1,0:T(4,128)S(1)}, f32[36,4,256]{2,1,0:T(4,128)S(1)}, u32[]{:S(2)}, u32[]{:S(2)}) collective-permute-start(f32[36,4,256]{2,1,0:T(4,128)S(1)} %get-tuple-element.24), channel_id=1, source_target_pairs={{0,1},{1,2},{2,3},{3,0},{4,5},{5,6},{6,7},{7,4},{8,9},{9,10},{10,1... | collective-permute-start | bytes 442376 | tf_op jit(solution)/shard_map/ppermute | solution.py:24
  4.9 0.0 collective-permute-start.2
  4.9 1.6 %collective-permute-start.5 = (f32[33,4,256]{2,1,0:T(4,128)S(1)}, f32[33,4,256]{2,1,0:T(4,128)S(1)}, u32[]{:S(2)}, u32[]{:S(2)}) collective-permute-start(f32[33,4,256]{2,1,0:T(4,128)S(1)} %get-tuple-element.31), channel_id=1, source_target_pairs={{0,1},{1,2},{2,3},{3,0},{4,5},{5,6},{6,7},{7,4},{8,9},{9,10},{10,1... | collective-permute-start | bytes 405512 | tf_op jit(solution)/shard_map/ppermute | solution.py:24
  6.4 2.2 %collective-permute-start.1 = (f32[33,4,256]{2,1,0:T(4,128)S(1)}, f32[33,4,256]{2,1,0:T(4,128)S(1)}, u32[]{:S(2)}, u32[]{:S(2)}) collective-permute-start(f32[33,4,256]{2,1,0:T(4,128)S(1)} %get-tuple-element.25), channel_id=1, source_target_pairs={{0,3},{1,0},{2,1},{3,2},{4,7},{5,4},{6,5},{7,6},{8,11},{9,8},{10,9... | collective-permute-start | bytes 405512 | tf_op jit(solution)/shard_map/ppermute | solution.py:24
  8.7 2.1 %collective-permute-start.3 = (f32[16,8,256]{2,1,0:T(8,128)S(1)}, f32[16,8,256]{2,1,0:T(8,128)S(1)}, u32[]{:S(2)}, u32[]{:S(2)}) collective-permute-start(f32[16,8,256]{2,1,0:T(8,128)S(1)} %get-tuple-element.27), channel_id=1, source_target_pairs={{0,28},{4,0},{8,4},{12,8},{16,12},{20,16},{24,20},{28,24},{1,29},{... | collective-permute-start | bytes 393224 | tf_op jit(solution)/shard_map/ppermute | solution.py:24
  10.8 2.8 %collective-permute-done.5 = f32[33,4,256]{2,1,0:T(4,128)S(1)} collective-permute-done((f32[33,4,256]{2,1,0:T(4,128)S(1)}, f32[33,4,256]{2,1,0:T(4,128)S(1)}, u32[]{:S(2)}, u32[]{:S(2)}) %collective-permute-start.5) | collective-permute-done | bytes 135200 | tf_op jit(solution)/shard_map/ppermute | solution.py:24
  13.6 4.7 %collective-permute-start.4 = (f32[31,4,256]{2,1,0:T(4,128)S(1)}, f32[31,4,256]{2,1,0:T(4,128)S(1)}, u32[]{:S(2)}, u32[]{:S(2)}) collective-permute-start(f32[31,4,256]{2,1,0:T(4,128)S(1)} %get-tuple-element.30), channel_id=1, source_target_pairs={{0,3},{1,0},{2,1},{3,2},{4,7},{5,4},{6,5},{7,6},{8,11},{9,8},{10,9... | collective-permute-start | bytes 380936 | tf_op jit(solution)/shard_map/ppermute | solution.py:24
  18.3 0.0 collective-permute-done.3.above
  18.3 0.0 collective-permute-done.1
  18.3 0.0 collective-permute-done.2.below
  18.3 0.0 collective-permute-done
  18.5 0.4 collective-permute-start.7
  18.8 0.7 %broadcast_select_fusion = f32[1,8,256]{2,1,0:T(8,128)S(1)} fusion(f32[1,8,256]{2,1,0:T(8,128)S(1)} %reshape.36, pred[8]{0:T(512)(128)(4,1)} %constant.3.clone.1), kind=kLoop, calls=%fused_computation.11 | loop fusion | flops 2048 | bytes 16392 | tf_op jit(solution)/shard_map/jit(_pad)/pad | solution.py:598
  19.6 0.3 collective-permute-start.6
  19.9 0.9 %collective-permute-done.4 = f32[31,4,256]{2,1,0:T(4,128)S(1)} collective-permute-done((f32[31,4,256]{2,1,0:T(4,128)S(1)}, f32[31,4,256]{2,1,0:T(4,128)S(1)}, u32[]{:S(2)}, u32[]{:S(2)}) %collective-permute-start.4) | collective-permute-done | bytes 127008 | tf_op jit(solution)/shard_map/ppermute | solution.py:24
  20.7 0.1 pad_maximum_fusion.1.side_b
  20.8 0.1 pad_maximum_fusion.side_a
  20.9 7.1 %inside.1 = (f32[5,3,16,8,256]{4,3,2,1,0:T(8,128)S(1)}, f32[16,8,256]{2,1,0:T(8,128)S(1)}, f32[16,16,256]{2,1,0:T(8,128)S(1)}, f32[4,3,4,16,256]{4,3,2,1,0:T(8,128)S(1)}, f32[1,128]{1,0:T(1,128)S(1)}) custom-call(f32[3,16,8,256]{3,2,1,0:T(8,128)S(1)} %get-tuple-element.22.r_own, f32[16,8,256]{2,1,0:T(8,128)S(1)} %get-tuple-element.23.lab_own, ...), custom_call_target="tpu_custom_call" | custom-call | tf_op jit(solution)/shard_map/inside/pallas_call | solution.py:626
  28.0 0.0 collective-permute-done.7.above_side
  28.0 0.0 collective-permute-done.6.below_side
  28.0 6.5 %finish.1 = (f32[5,3,16,8,256]{4,3,2,1,0:T(8,128)S(1)}, f32[8,256]{1,0:T(8,128)S(1)}, f32[32,1,128]{2,1,0:T(1,128)S(1)}) custom-call(f32[3,16,8,256]{3,2,1,0:T(8,128)S(1)} %get-tuple-element.22.r_own, f32[16,8,256]{2,1,0:T(8,128)S(1)} %get-tuple-element.23.lab_own, f32[33,8,256]{2,1,0:T(8,128)S(1)} %pad_maximum_fusion.side_a, ...), custom_call_target="tpu_custom_call" | custom-call | tf_op jit(solution)/shard_map/finish/pallas_call | solution.py:645
  34.6 13.5 %all_to_all.5 = f32[32,1,128]{2,1,0:T(1,128)S(1)} all-to-all(f32[32,1,128]{2,1,0:T(1,128)S(1)} %get-tuple-element.38), channel_id=1, replica_groups=mesh['gx'=8,'gy'=4] {'gx','gy'}, dimensions={0} | all-to-all | bytes 32768 | tf_op jit(solution)/shard_map/all_to_all | solution.py:664
  48.1 1.3 %combine.1 = (f32[3,16,8,256]{3,2,1,0:T(8,128)}, f32[3,16,8,256]{3,2,1,0:T(8,128)}) custom-call(f32[32,128]{1,0:T(8,128)S(1)} %bitcast.3, f32[5,3,16,8,256]{4,3,2,1,0:T(8,128)S(1)} %get-tuple-element.34.t_in.inner_ref, f32[5,3,16,8,256]{4,3,2,1,0:T(8,128)S(1)} %get-tuple-element.39.outer_ref, f32[16,8,256]{2,1,0:T(8,128)S(1)} %get-tuple-element.40.d_inner, ...), custom_call_target="tpu_custom_call" | custom-call | tf_op jit(solution)/shard_map/combine/pallas_call | solution.py:666
  (14 shorter events, 0.2 us)
Async XLA Ops:
  1.8 16.6 %collective-permute-start = (f32[36,4,256]{2,1,0:T(4,128)S(1)}, f32[36,4,256]{2,1,0:T(4,128)S(1)}, u32[]{:S(2)}, u32[]{:S(2)}) collective-permute-start(f32[36,4,256]{2,1,0:T(4,128)S(1)} %get-tuple-element.24), channel_id=1, source_target_pairs={{0,1},{1,2},{2,3},{3,0},{4,5},{5,6},{6,7},{7,4},{8,9},{9,10},{10,1... | collective-permute-start | bytes 442376 | tf_op jit(solution)/shard_map/ppermute | solution.py:24
  4.9 13.4 %collective-permute-start.2 = (f32[17,8,256]{2,1,0:T(8,128)S(1)}, f32[17,8,256]{2,1,0:T(8,128)S(1)}, u32[]{:S(2)}, u32[]{:S(2)}) collective-permute-start(f32[17,8,256]{2,1,0:T(8,128)S(1)} %get-tuple-element.26), channel_id=1, source_target_pairs={{0,4},{4,8},{8,12},{12,16},{16,20},{20,24},{24,28},{28,0},{1,5},{5... | collective-permute-start | bytes 417800 | tf_op jit(solution)/shard_map/ppermute | solution.py:24
  4.9 8.7 %collective-permute-start.5 = (f32[33,4,256]{2,1,0:T(4,128)S(1)}, f32[33,4,256]{2,1,0:T(4,128)S(1)}, u32[]{:S(2)}, u32[]{:S(2)}) collective-permute-start(f32[33,4,256]{2,1,0:T(4,128)S(1)} %get-tuple-element.31), channel_id=1, source_target_pairs={{0,1},{1,2},{2,3},{3,0},{4,5},{5,6},{6,7},{7,4},{8,9},{9,10},{10,1... | collective-permute-start | bytes 405512 | tf_op jit(solution)/shard_map/ppermute | solution.py:24
  6.4 11.9 %collective-permute-start.1 = (f32[33,4,256]{2,1,0:T(4,128)S(1)}, f32[33,4,256]{2,1,0:T(4,128)S(1)}, u32[]{:S(2)}, u32[]{:S(2)}) collective-permute-start(f32[33,4,256]{2,1,0:T(4,128)S(1)} %get-tuple-element.25), channel_id=1, source_target_pairs={{0,3},{1,0},{2,1},{3,2},{4,7},{5,4},{6,5},{7,6},{8,11},{9,8},{10,9... | collective-permute-start | bytes 405512 | tf_op jit(solution)/shard_map/ppermute | solution.py:24
  8.7 9.6 %collective-permute-start.3 = (f32[16,8,256]{2,1,0:T(8,128)S(1)}, f32[16,8,256]{2,1,0:T(8,128)S(1)}, u32[]{:S(2)}, u32[]{:S(2)}) collective-permute-start(f32[16,8,256]{2,1,0:T(8,128)S(1)} %get-tuple-element.27), channel_id=1, source_target_pairs={{0,28},{4,0},{8,4},{12,8},{16,12},{20,16},{24,20},{28,24},{1,29},{... | collective-permute-start | bytes 393224 | tf_op jit(solution)/shard_map/ppermute | solution.py:24
  13.6 7.1 %collective-permute-start.4 = (f32[31,4,256]{2,1,0:T(4,128)S(1)}, f32[31,4,256]{2,1,0:T(4,128)S(1)}, u32[]{:S(2)}, u32[]{:S(2)}) collective-permute-start(f32[31,4,256]{2,1,0:T(4,128)S(1)} %get-tuple-element.30), channel_id=1, source_target_pairs={{0,3},{1,0},{2,1},{3,2},{4,7},{5,4},{6,5},{7,6},{8,11},{9,8},{10,9... | collective-permute-start | bytes 380936 | tf_op jit(solution)/shard_map/ppermute | solution.py:24
  18.5 9.6 %collective-permute-start.7 = (f32[17,8,256]{2,1,0:T(8,128)S(1)}, f32[17,8,256]{2,1,0:T(8,128)S(1)}, u32[]{:S(2)}, u32[]{:S(2)}) collective-permute-start(f32[17,8,256]{2,1,0:T(8,128)S(1)} %pad_maximum_fusion.3), channel_id=1, source_target_pairs={{0,28},{4,0},{8,4},{12,8},{16,12},{20,16},{24,20},{28,24},{1,29},{... | collective-permute-start | bytes 417800 | tf_op jit(solution)/shard_map/ppermute | solution.py:24
  19.6 8.4 %collective-permute-start.6 = (f32[18,8,256]{2,1,0:T(8,128)S(1)}, f32[18,8,256]{2,1,0:T(8,128)S(1)}, u32[]{:S(2)}, u32[]{:S(2)}) collective-permute-start(f32[18,8,256]{2,1,0:T(8,128)S(1)} %pad_maximum_fusion.2), channel_id=1, source_target_pairs={{0,4},{4,8},{8,12},{12,16},{16,20},{20,24},{24,28},{28,0},{1,5},{5... | collective-permute-start | bytes 442376 | tf_op jit(solution)/shard_map/ppermute | solution.py:24
where the time goes:
time: 49.5 us; the launch traced here: 49.4 us
  Pallas kernels  16.1 us (33%)
  starting transfers between devices  14.3 us (29%)
  blocking collectives  13.5 us (27%)
  waiting for transfers between devices  3.73 us (8%)
  other arithmetic  0.92 us (2%)
  between operations  0.8 us (2%)
    ppermute x8, starting transfers between devices, shifted(): lax.ppermute(shard, axis, [(i, (i + by) % size) for i in range(size)])  14.3 us
    all_to_all x1, blocking collectives, local(): everyone = lax.all_to_all(sums, ('gx', 'gy'), 0, 0)  13.5 us
    pallas_call x1, Pallas kernels, local(): pl.pallas_call(inside_kernel, out_shape=(own_basis, jax.ShapeDtypeStruct(...  7.13 us
    pallas_call x1, Pallas kernels, local(): pl.pallas_call(finish_kernel, out_shape=(own_basis, jax.ShapeDtypeStruct(...  6.54 us
    ppermute x8, waiting for transfers between devices, shifted(): lax.ppermute(shard, axis, [(i, (i + by) % size) for i in range(size)])  3.73 us
    pallas_call x1, Pallas kernels, local(): pl.pallas_call(combine_kernel, out_shape=(out, out), compiler_params=smal...  1.27 us
    pallas_call x1, Pallas kernels, local(): pl.pallas_call(pack_kernel, out_shape=(jax.ShapeDtypeStruct(right_side.sh...  1.11 us
  transfers between devices with their start and end apart: 8, of which 2 were waited for; matrix products, arithmetic and copies ran while one was open for 2% of the time, Pallas kernels for 14%

commit v1 on v0

--- a/solution.py
+++ b/solution.py
@@ -180,7 +180,11 @@
         return far, ahead
 
     near = [q_ref[first, i, j] for i in range(len(MODES))]
-    pairs(first, last, voxels, (near, [jnp.zeros_like(v) for v in near]))
+    carry = near, [jnp.zeros_like(v) for v in near]
+    even = first + (last - first) // 2 * 2
+    carry = pairs(first, even, voxels, carry)
+    for n in range(even, last):
+        carry = voxels(n, carry)
 
 
 def collect(n, f_ref, image_ref):
@@ -245,15 +249,12 @@
     return node, cell, edge, blocks, edge_blocks
 
 
-def inside_kernel(
+def begin_kernel(
     r_own, lab_own, side_a, side_b, edge_a, edge_b,
-    t_out, d_out, inv_out, edge_out, sums_out,
-    side_ref, edge_ref, t_ref, turn_ref, image_ref, q_ref, f_ref,
+    side_out, t_out, inv_out, d_out,
+    edge_ref, turn_ref,
 ):
     own_x, own_y, depth = r_own.shape[1:]
-    rows = own_y + side_ref.shape[2]
-    tiles = tiles_of(rows, depth)
-    count = own_x - 1
 
     def both(block, side):
         return jnp.concatenate([block, side], 0)
@@ -263,99 +264,46 @@
     for x in range(own_x):
         for comp in range(3):
             part, place = node_at(comp, x)
-            side_ref[comp, x] = sides[part][place]
+            side_out[comp, x] = sides[part][place]
         part, place = cell_at(x)
-        side_ref[3, x] = sides[part][place]
+        side_out[3, x] = sides[part][place]
         part, place = edge_at(x)
         edge_ref[x : x + 1] = edges[part][place : place + 1]
     lines = edge_ref[...]
     edge_ref[...] = lines + roll(lines, 1, 1)
     for m in range(own_x):
-        put(turn_ref, 0, m, value=roll(both(lab_own[m], side_ref[3, m]), 1, 1))
+        turn_ref[m] = roll(both(lab_own[m], side_out[3, m]), 1, 1)
 
     def layer(m):
-        cells = both(lab_own[m], side_ref[3, m])
-        return diagonal_layer(cells, get(turn_ref, 0, m), edge_ref[pl.ds(m, 1), :], own_y + HALO)
-
-    def start(p, before):
-        here = layer(p + 1)
+        cells = both(lab_own[m], side_out[3, m])
+        return diagonal_layer(cells, turn_ref[m], edge_ref[pl.ds(m, 1), :], own_y + HALO)
+
+    def start(x, before):
+        here = layer(x)
         diag = diagonal_from(before + here)
         inv = 1.0 / diag
-        inv_out[p + 1] = inv
-        d_out[p + 1] = diag[:own_y]
+        inv_out[x] = inv
+        d_out[x] = diag[:own_y]
         for comp in range(3):
-            t = both(r_own[comp, p + 1], side_ref[comp, p + 1]) * inv
-            put(t_ref, 0, comp, p, value=t)
-            t_out[0, comp, p + 1] = t[:own_y]
+            put(t_out, comp, x, value=both(r_own[comp, x], side_out[comp, x]) * inv)
         return here
 
-    before = pairs(0, count - 1, start, layer(0))
-    start(count - 1, before)
-
-    totals = []
-    for k in range(ITERS):
-        first, last = k, count - k
-        for i, p in enumerate((first, first + 1, last - 2, last - 1)):
-            for comp in range(3):
-                edge_out[k, comp, i] = get(t_ref, k, comp, p)
-        forward_planes(first, last, t_ref.at[k], turn_ref, q_ref)
-        for j, (line, lanes) in enumerate(tiles):
-
-            def cells_at(n):
-                if line.start < own_y:
-                    return lab_own[n + 1, line, lanes]
-                return side_ref[3, n + 1, line.start - own_y : line.stop - own_y, lanes]
-
-            voxel_layers(j, first, last - 1, cells_at, q_ref, f_ref)
-
-        def advance(p, acc):
-            acc = list(acc)
-            new = update(k, inv_out[p + 1])
-            for comp in range(3):
-                t = get(t_ref, k, comp, p)
-                force = image_ref[comp, p]
-                image = force[:own_y] + KAPPA * t[:own_y]
-                for j in range(k + 1):
-                    acc[j] += get(t_ref, j, comp, p, rows=own_y) * image
-                acc[k + 1] += t[:own_y] * r_own[comp, p + 1]
-                t = new(force, t, lambda: get(t_ref, k - 1, comp, p))
-                if k + 1 < ITERS:
-                    put(t_ref, k + 1, comp, p, value=t)
-                t_out[k + 1, comp, p + 1] = t[:own_y]
-            return tuple(acc)
-
-        def several(n, acc):
-            for u in range(WIDTH):
-                acc = advance(n + u, acc)
-            for u in range(WIDTH):
-                collect(n + WIDTH + u, f_ref, image_ref)
-            return acc
-
-        begin, end = first + 1, last - 1
-        whole = begin + (end - begin) // WIDTH * WIDTH
-        for p in range(begin, begin + WIDTH):
-            collect(p, f_ref, image_ref)
-        acc = (jnp.zeros((own_y, depth), jnp.float32),) * (k + 2)
-        acc = strides(begin, whole, WIDTH, several, acc)
-        for p in range(whole, end):
-            acc = advance(p, acc)
-        totals.extend(acc)
-    sums_out[...] = packed_sums(totals)
-
-
-def finish_kernel(
-    r_own, lab_own, side_a, side_b, edge_a, below, above, below_side, above_side,
-    t_in, inv_in, edge_in, sums_in,
+    before = pairs(1, own_x - 1, start, layer(0))
+    start(own_x - 1, before)
+
+
+def basis_kernel(
+    r_own, lab_own, side_ref, edge_a, below, above, below_side, above_side, t0_in, inv_in,
     t_out, d_out, sums_out,
-    cell_ref, inv_ref, u_ref, turn_ref, image_ref, q_ref, f_ref,
+    cell_ref, inv_ref, t_ref, turn_ref, image_ref, q_ref, f_ref,
 ):
     h = HALO
     own_x, own_y, depth = r_own.shape[1:]
-    rows = own_y + side_a.shape[1]
+    rows = own_y + side_ref.shape[2]
     tiles = tiles_of(rows, depth)
-    left, right = h + 3, h + 2
-    node_at, cell_at, edge_at = y_parts(own_x)[:3]
-    sides = (side_a, side_b)
+    planes = own_x + 2 * h
+    lo, hi = h, h + own_x
+    edge_at = y_parts(own_x)[2]
 
     def nodes(comp, x):
         if x < 0:
@@ -363,18 +311,7 @@
         if x >= own_x:
             i = comp * h + x - own_x
             return jnp.concatenate([above[i], above_side[i]], 0)
-        part, place = node_at(comp, x)
-        return jnp.concatenate([r_own[comp, x], sides[part][place]], 0)
-
-    def cells(x):
-        if x < 0:
-            i = 3 * h + h + 1 + x
-            return jnp.concatenate([below[i], below_side[i]], 0)
-        if x >= own_x:
-            i = 3 * h + x - own_x
-            return jnp.concatenate([above[i], above_side[i]], 0)
-        part, place = cell_at(x)
-        return jnp.concatenate([lab_own[x], sides[part][place]], 0)
+        return jnp.concatenate([r_own[comp, x], side_ref[comp, x]], 0)
 
     def edge(x):
         if x < 0:
@@ -384,16 +321,26 @@
         place = edge_at(x)[1]
         return edge_a[place : place + 1]
 
-    for x in [*range(-h - 1, ITERS + 1), *range(own_x - 1 - ITERS, own_x + h)]:
-        cell_ref[x + h + 1] = cells(x)
+    for i in range(h + 1):
+        cell_ref[i] = jnp.concatenate([below[3 * h + i], below_side[3 * h + i]], 0)
+    for i in range(h):
+        cell_ref[h + 1 + own_x + i] = jnp.concatenate([above[3 * h + i], above_side[3 * h + i]], 0)
+
+    def copy(x, _):
+        cell_ref[x + h + 1] = jnp.concatenate([lab_own[x], side_ref[3, x]], 0)
+        inv_ref[x + h] = inv_in[x]
+        for comp in range(3):
+            t = get(t0_in, comp, x)
+            put(t_ref, 0, comp, x + h, value=t)
+            t_out[0, comp, x] = t[:own_y]
+        return _
+
+    pairs(0, own_x, copy, 0)
 
     def layer(x):
         e = edge(x)
         c = cell_ref[x + h + 1]
         return diagonal_layer(c, roll(c, 1, 1), e + roll(e, 1, 1), own_y + h)
-
-    def place(k, x):
-        return x - (k - h) if x < own_x // 2 else left + x - (own_x - 2 - k)
 
     for start, stop in ((-h, 1), (own_x, own_x + h)):
         layers = [layer(x) for x in range(start - 1, stop)]
@@ -405,52 +352,54 @@
                 d_out[...] = diag[:own_y]
             for comp in range(3):
                 t = nodes(comp, x) * inv
-                put(u_ref, 0, comp, place(0, x), value=t)
+                put(t_ref, 0, comp, x + h, value=t)
                 if x == 0:
                     t_out[0, comp, 0] = t[:own_y]
-    for x in [*range(1, ITERS + 1), *range(own_x - ITERS, own_x)]:
-        inv_ref[x + h] = inv_in[x]
-
-    def own_rows(j, comp, x):
-        ref = t_out if x <= j or x >= own_x - j else t_in
-        return ref[j, comp, x]
 
     totals = []
     for k in range(ITERS):
-        for comp in range(3):
-            for i, p in enumerate((left - 2, left - 1, left, left + 1)):
-                put(u_ref, k, comp, p, value=edge_in[k, comp, i])
-        forward_planes(0, left + right, u_ref.at[k], turn_ref, q_ref)
+        first, last = k, planes - k
+        forward_planes(first, last, t_ref.at[k], turn_ref, q_ref)
         for j, (line, lanes) in enumerate(tiles):
-            voxel_layers(j, 0, left - 1, lambda n: cell_ref[n + k + 1, line, lanes], q_ref, f_ref)
-            shift = own_x - 2 - k - left + h + 1
-            voxel_layers(
-                j, left, left + right - 1, lambda n: cell_ref[n + shift, line, lanes], q_ref, f_ref
-            )
-        planes = [*range(k - h + 1, k + 2), *range(own_x - 1 - k, own_x + h - 1 - k)]
-        if k + 1 == ITERS:
-            planes = [x for x in planes if 0 <= x < own_x]
-        for x in planes:
-            collect(place(k, x), f_ref, image_ref)
-        acc = [jnp.zeros((own_y, depth), jnp.float32)] * (k + 2)
-        for x in planes:
-            new = update(k, inv_ref[x + h])
-            own = 0 <= x < own_x
+            voxel_layers(j, first, last - 1, lambda n: cell_ref[n + 1, line, lanes], q_ref, f_ref)
+
+        def advance(n, own, acc):
+            acc = list(acc)
+            new = update(k, inv_ref[n])
             for comp in range(3):
-                t = get(u_ref, k, comp, place(k, x))
-                force = image_ref[comp, place(k, x)]
+                t = get(t_ref, k, comp, n)
+                force = image_ref[comp, n]
                 if own:
                     image = force[:own_y] + KAPPA * t[:own_y]
                     for j in range(k + 1):
-                        acc[j] += own_rows(j, comp, x) * image
-                    acc[k + 1] += t[:own_y] * r_own[comp, x]
-                t = new(force, t, lambda: get(u_ref, k - 1, comp, place(k - 1, x)))
+                        acc[j] += get(t_ref, j, comp, n, rows=own_y) * image
+                    acc[k + 1] += t[:own_y] * r_own[comp, n - lo]
+                t = new(force, t, lambda: get(t_ref, k - 1, comp, n))
                 if k + 1 < ITERS:
-                    put(u_ref, k + 1, comp, place(k + 1, x), value=t)
+                    put(t_ref, k + 1, comp, n, value=t)
                 if own:
-                    t_out[k + 1, comp, x] = t[:own_y]
+                    t_out[k + 1, comp, n - lo] = t[:own_y]
+            return tuple(acc)
+
+        def several(n, acc):
+            for u in range(WIDTH):
+                acc = advance(n + u, True, acc)
+            for u in range(WIDTH):
+                collect(n + WIDTH + u, f_ref, image_ref)
+            return acc
+
+        beside = [*range(first + 1, lo), *range(hi, last - 1)] if k + 1 < ITERS else []
+        for n in [*beside, *range(lo, lo + WIDTH)]:
+            collect(n, f_ref, image_ref)
+        for n in beside:
+            advance(n, False, ())
+        acc = (jnp.zeros((own_y, depth), jnp.float32),) * (k + 2)
+        whole = lo + own_x // WIDTH * WIDTH
+        acc = strides(lo, whole, WIDTH, several, acc)
+        for n in range(whole, hi):
+            acc = advance(n, True, acc)
         totals.extend(acc)
-    sums_out[...] = jnp.broadcast_to((packed_sums(totals) + sums_in[...])[None], sums_out.shape)
+    sums_out[...] = jnp.broadcast_to(packed_sums(totals)[None], sums_out.shape)
 
 
 def pack_kernel(
@@ -492,7 +441,7 @@
                 next_out[comp * h + x - (own_x - h)] = r
 
 
-def combine_kernel(sums_ref, inner_ref, outer_ref, d_inner, d_outer, x_out, r_out):
+def combine_kernel(sums_ref, t_ref, d_ref, d_first, x_out, r_out):
     total = jnp.sum(sums_ref[...], axis=0, keepdims=True)
     lane = lax.broadcasted_iota(jnp.int32, total.shape, 1)
     entry = [
@@ -529,18 +478,12 @@
         e[k] = e[k] - SHIFT[k] * y[k]
         if k > 1:
             e[k - 1] = e[k - 1] - STEP[k - 1] * y[k]
-    y = [jnp.broadcast_to(v, d_outer.shape) for v in y]
-    e = [jnp.broadcast_to(v, d_outer.shape) for v in e]
-
-    own_x = d_inner.shape[0]
-
-    def plane(n, outer):
-        diag = d_inner[n] if outer is None or n > 0 else d_outer[...]
+    y = [jnp.broadcast_to(v, d_first.shape) for v in y]
+    e = [jnp.broadcast_to(v, d_first.shape) for v in e]
+
+    def plane(n, diag):
         for comp in range(3):
-            t = []
-            for k in range(ITERS + 1):
-                edge = outer is not None and (n <= k or n >= own_x - k)
-                t.append((outer_ref if edge else inner_ref)[k, comp, n])
+            t = [t_ref[k, comp, n] for k in range(ITERS + 1)]
             x, r = y[0] * t[0], e[0] * t[0]
             for k in range(1, ITERS):
                 x = x + y[k] * t[k]
@@ -549,14 +492,13 @@
             x_out[comp, n] = x
             r_out[comp, n] = r * diag
 
-    for n in [*range(ITERS + 1), *range(own_x - ITERS, own_x)]:
-        plane(n, True)
-
     def body(n, _):
-        plane(n, None)
+        plane(n, d_ref[n])
         return _
 
-    lax.fori_loop(ITERS + 1, own_x - ITERS, body, 0)
+    plane(0, d_first[...])
+    pairs(1, d_ref.shape[0] - 1, body, 0)
+    plane(d_ref.shape[0] - 1, d_ref[d_ref.shape[0] - 1])
 
 
 def local(right_side, labels):
@@ -621,50 +563,43 @@
             kept(planes, len(MODES)),
         ]
 
-    planes = own_x + 2 * WIDTH
-    own_basis = jax.ShapeDtypeStruct((ITERS + 1, 3, own_x, own_y, depth), f32)
-    inner, d_inner, inverse, borders, inner_sums = pl.pallas_call(
-        inside_kernel,
+    side, t0, inverse, diagonal = pl.pallas_call(
+        begin_kernel,
         out_shape=(
-            own_basis,
+            jax.ShapeDtypeStruct((4, own_x, 2 * h, depth), f32),
+            jax.ShapeDtypeStruct((3, own_x, across, rows + 8, 128), f32),
+            jax.ShapeDtypeStruct((own_x, rows, depth), f32),
             jax.ShapeDtypeStruct((own_x, own_y, depth), f32),
-            jax.ShapeDtypeStruct((own_x, rows, depth), f32),
-            jax.ShapeDtypeStruct((ITERS, 3, 4, rows, depth), f32),
-            jax.ShapeDtypeStruct((1, 128), f32),
         ),
         scratch_shapes=[
-            pltpu.VMEM((4, own_x, 2 * h, depth), f32),
             pltpu.VMEM((own_x, depth), f32),
-            *scratch(planes),
+            pltpu.VMEM((own_x, rows, depth), f32),
         ],
-        compiler_params=pltpu.CompilerParams(vmem_limit_bytes=28 * 2**20),
-        name="inside",
+        compiler_params=small,
+        name="begin",
     )(right_side, lab, side_a, side_b, edge_a, edge_b)
 
-    strips = 4 * h + 12
-    outer, d_outer, sums = pl.pallas_call(
-        finish_kernel,
+    planes = own_x + 2 * h
+    basis, d_first, sums = pl.pallas_call(
+        basis_kernel,
         out_shape=(
-            own_basis,
+            jax.ShapeDtypeStruct((ITERS + 1, 3, own_x, own_y, depth), f32),
             jax.ShapeDtypeStruct((own_y, depth), f32),
             jax.ShapeDtypeStruct((devices, 1, 128), f32),
         ),
         scratch_shapes=[
-            pltpu.VMEM((own_x + 2 * h + 2, rows, depth), f32),
-            pltpu.VMEM((own_x + 2 * h, rows, depth), f32),
-            *scratch(strips),
+            pltpu.VMEM((planes + 2, rows, depth), f32),
+            pltpu.VMEM((planes, rows, depth), f32),
+            *scratch(planes + 1),
         ],
-        compiler_params=pltpu.CompilerParams(vmem_limit_bytes=28 * 2**20),
-        name="finish",
-    )(
-        right_side, lab, side_a, side_b, edge_a, below, above, below_side, above_side,
-        inner, inverse, borders, inner_sums,
-    )
+        compiler_params=pltpu.CompilerParams(vmem_limit_bytes=34 * 2**20),
+        name="basis",
+    )(right_side, lab, side, edge_a, below, above, below_side, above_side, t0, inverse)
 
     everyone = lax.all_to_all(sums, ("gx", "gy"), 0, 0)
     out = jax.ShapeDtypeStruct(right_side.shape, f32)
     return pl.pallas_call(combine_kernel, out_shape=(out, out), compiler_params=small, name="combine")(
-        everyone.reshape(devices, 128), inner, outer, d_inner, d_outer
+        everyone.reshape(devices, 128), basis, diagonal, d_first
     )
 
 

time: 49.5 us -> 48.6 us (0.982)
  waiting for transfers between devices: 3.73 us -> 8.03 us
  blocking collectives: 13.5 us -> 9.22 us
  Pallas kernels: 16.1 us -> 15.1 us
    ppermute x8, waiting for transfers between devices: 3.73 us -> 8.03 us  [shifted(): lax.ppermute(shard, axis, [(i, (i + by) % size) for i in range(size)])]
    all_to_all x1, blocking collectives: 13.5 us -> 9.22 us  [local(): everyone = lax.all_to_all(sums, ('gx', 'gy'), 0, 0)]
    pallas_call x2, Pallas kernels: 13.7 us -> 12.7 us  [the longest x1 12.3 us: local(): pl.pallas_call(basis_kernel, out_shape=(jax.ShapeDtypeStruct((ITERS + 1,...]
  transfers between devices with their start and end apart: 8 -> 8, of which waited for: 2 -> 4; matrix products, arithmetic and copies ran while one was open for 2% -> 2% of each run, Pallas kernels for 14% -> 1%
where the time goes in v1:
time: 48.6 us; the launch traced here: 48.4 us
  Pallas kernels  15.1 us (31%)
  starting transfers between devices  14.3 us (29%)
  blocking collectives  9.22 us (19%)
  waiting for transfers between devices  8.03 us (17%)
  other arithmetic  0.92 us (2%)
  between operations  0.79 us (2%)
    ppermute x8, starting transfers between devices, shifted(): lax.ppermute(shard, axis, [(i, (i + by) % size) for i in range(size)])  14.3 us
    pallas_call x1, Pallas kernels, local(): pl.pallas_call(basis_kernel, out_shape=(jax.ShapeDtypeStruct((ITERS + 1,...  12.3 us
    all_to_all x1, blocking collectives, local(): everyone = lax.all_to_all(sums, ('gx', 'gy'), 0, 0)  9.22 us
    ppermute x8, waiting for transfers between devices, shifted(): lax.ppermute(shard, axis, [(i, (i + by) % size) for i in range(size)])  8.03 us
    pallas_call x1, Pallas kernels, local(): pl.pallas_call(combine_kernel, out_shape=(out, out), compiler_params=smal...  1.26 us
    pallas_call x1, Pallas kernels, local(): pl.pallas_call(pack_kernel, out_shape=(jax.ShapeDtypeStruct(right_side.sh...  1.11 us
  transfers between devices with their start and end apart: 8, of which 4 were waited for; matrix products, arithmetic and copies ran while one was open for 2% of the time, Pallas kernels for 1%

profile of v1, /device:TPU:0, one launch (start us, length us, event | category | flops | bytes accessed | tf_op | source)
XLA Modules:
  0.0 48.4 jit_solution(9071389576457606194)
XLA Ops:
  0.6 1.1 %pack.1 = (f32[3,16,8,256]{3,2,1,0:T(8,128)S(1)}, f32[16,8,256]{2,1,0:T(8,128)S(1)}, f32[36,4,256]{2,1,0:T(4,128)S(1)}, f32[33,4,256]{2,1,0:T(4,128)S(1)}, f32[3...) custom-call(f32[3,16,8,256]{3,2,1,0:T(8,128)} %r_hbm.1, ...), custom_call_target="tpu_custom_call" | custom-call | tf_op jit(solution)/shard_map/pack/pallas_call | solution.py:511
  1.7 3.1 %collective-permute-start = (f32[36,4,256]{2,1,0:T(4,128)S(1)}, f32[36,4,256]{2,1,0:T(4,128)S(1)}, u32[]{:S(2)}, u32[]{:S(2)}) collective-permute-start(f32[36,4,256]{2,1,0:T(4,128)S(1)} %get-tuple-element.23), channel_id=1, source_target_pairs={{0,1},{1,2},{2,3},{3,0},{4,5},{5,6},{6,7},{7,4},{8,9},{9,10},{10,1... | collective-permute-start | bytes 442376 | tf_op jit(solution)/shard_map/ppermute | solution.py:24
  4.8 0.0 collective-permute-start.2
  4.9 1.6 %collective-permute-start.5 = (f32[33,4,256]{2,1,0:T(4,128)S(1)}, f32[33,4,256]{2,1,0:T(4,128)S(1)}, u32[]{:S(2)}, u32[]{:S(2)}) collective-permute-start(f32[33,4,256]{2,1,0:T(4,128)S(1)} %get-tuple-element.30), channel_id=1, source_target_pairs={{0,1},{1,2},{2,3},{3,0},{4,5},{5,6},{6,7},{7,4},{8,9},{9,10},{10,1... | collective-permute-start | bytes 405512 | tf_op jit(solution)/shard_map/ppermute | solution.py:24
  6.4 2.2 %collective-permute-start.1 = (f32[33,4,256]{2,1,0:T(4,128)S(1)}, f32[33,4,256]{2,1,0:T(4,128)S(1)}, u32[]{:S(2)}, u32[]{:S(2)}) collective-permute-start(f32[33,4,256]{2,1,0:T(4,128)S(1)} %get-tuple-element.24), channel_id=1, source_target_pairs={{0,3},{1,0},{2,1},{3,2},{4,7},{5,4},{6,5},{7,6},{8,11},{9,8},{10,9... | collective-permute-start | bytes 405512 | tf_op jit(solution)/shard_map/ppermute | solution.py:24
  8.7 2.1 %collective-permute-start.3 = (f32[16,8,256]{2,1,0:T(8,128)S(1)}, f32[16,8,256]{2,1,0:T(8,128)S(1)}, u32[]{:S(2)}, u32[]{:S(2)}) collective-permute-start(f32[16,8,256]{2,1,0:T(8,128)S(1)} %get-tuple-element.26), channel_id=1, source_target_pairs={{0,28},{4,0},{8,4},{12,8},{16,12},{20,16},{24,20},{28,24},{1,29},{... | collective-permute-start | bytes 393224 | tf_op jit(solution)/shard_map/ppermute | solution.py:24
  10.8 2.8 %collective-permute-done.5 = f32[33,4,256]{2,1,0:T(4,128)S(1)} collective-permute-done((f32[33,4,256]{2,1,0:T(4,128)S(1)}, f32[33,4,256]{2,1,0:T(4,128)S(1)}, u32[]{:S(2)}, u32[]{:S(2)}) %collective-permute-start.5) | collective-permute-done | bytes 135200 | tf_op jit(solution)/shard_map/ppermute | solution.py:24
  13.6 4.7 %collective-permute-start.4 = (f32[31,4,256]{2,1,0:T(4,128)S(1)}, f32[31,4,256]{2,1,0:T(4,128)S(1)}, u32[]{:S(2)}, u32[]{:S(2)}) collective-permute-start(f32[31,4,256]{2,1,0:T(4,128)S(1)} %get-tuple-element.29), channel_id=1, source_target_pairs={{0,3},{1,0},{2,1},{3,2},{4,7},{5,4},{6,5},{7,6},{8,11},{9,8},{10,9... | collective-permute-start | bytes 380936 | tf_op jit(solution)/shard_map/ppermute | solution.py:24
  18.3 0.0 collective-permute-done.3.above
  18.3 0.0 collective-permute-done.1
  18.3 0.0 collective-permute-done.2.below
  18.3 0.0 collective-permute-done
  18.5 0.4 collective-permute-start.7
  18.8 0.7 %broadcast_select_fusion = f32[1,8,256]{2,1,0:T(8,128)S(1)} fusion(f32[1,8,256]{2,1,0:T(8,128)S(1)} %reshape.37, pred[8]{0:T(512)(128)(4,1)} %constant.3.clone.1), kind=kLoop, calls=%fused_computation.11 | loop fusion | flops 2048 | bytes 16392 | tf_op jit(solution)/shard_map/jit(_pad)/pad | solution.py:540
  19.6 0.3 collective-permute-start.6
  19.9 0.9 %collective-permute-done.4 = f32[31,4,256]{2,1,0:T(4,128)S(1)} collective-permute-done((f32[31,4,256]{2,1,0:T(4,128)S(1)}, f32[31,4,256]{2,1,0:T(4,128)S(1)}, u32[]{:S(2)}, u32[]{:S(2)}) %collective-permute-start.4) | collective-permute-done | bytes 127008 | tf_op jit(solution)/shard_map/ppermute | solution.py:24
  20.7 0.1 pad_maximum_fusion.1.side_b
  20.8 0.1 pad_maximum_fusion.side_a
  20.9 0.4 begin.1
  21.3 0.2 collective-permute-done.7.above_side
  21.4 4.2 %collective-permute-done.6.below_side = f32[18,8,256]{2,1,0:T(8,128)S(1)} collective-permute-done((f32[18,8,256]{2,1,0:T(8,128)S(1)}, f32[18,8,256]{2,1,0:T(8,128)S(1)}, u32[]{:S(2)}, u32[]{:S(2)}) %collective-permute-start.6) | collective-permute-done | bytes 147488 | tf_op jit(solution)/shard_map/ppermute | solution.py:24
  25.6 12.3 %basis.1 = (f32[5,3,16,8,256]{4,3,2,1,0:T(8,128)S(1)}, f32[8,256]{1,0:T(8,128)S(1)}, f32[32,1,128]{2,1,0:T(1,128)S(1)}) custom-call(f32[3,16,8,256]{3,2,1,0:T(8,128)S(1)} %get-tuple-element.21.r_own, f32[16,8,256]{2,1,0:T(8,128)S(1)} %get-tuple-element.22.lab_own, f32[4,16,8,256]{3,2,1,0:T(8,128)S(1)} %get-tuple-element.31.side_ref, ...), custom_call_target="tpu_custom_call" | custom-call | tf_op jit(solution)/shard_map/basis/pallas_call | solution.py:583
  37.9 9.2 %all_to_all.5 = f32[32,1,128]{2,1,0:T(1,128)S(1)} all-to-all(f32[32,1,128]{2,1,0:T(1,128)S(1)} %get-tuple-element.36), channel_id=1, replica_groups=mesh['gx'=8,'gy'=4] {'gx','gy'}, dimensions={0} | all-to-all | bytes 32768 | tf_op jit(solution)/shard_map/all_to_all | solution.py:599
  47.1 1.3 %combine.1 = (f32[3,16,8,256]{3,2,1,0:T(8,128)}, f32[3,16,8,256]{3,2,1,0:T(8,128)}) custom-call(f32[32,128]{1,0:T(8,128)S(1)} %bitcast.3, f32[5,3,16,8,256]{4,3,2,1,0:T(8,128)S(1)} %get-tuple-element.37.t_ref, f32[16,8,256]{2,1,0:T(8,128)S(1)} %get-tuple-element.38.d_ref, f32[8,256]{1,0:T(8,128)S(1)} %get-tuple-element.39.d_first), custom_call_target="tpu_custom_call" | custom-call | tf_op jit(solution)/shard_map/combine/pallas_call | solution.py:601
  (14 shorter events, 0.2 us)
Async XLA Ops:
  1.7 16.6 %collective-permute-start = (f32[36,4,256]{2,1,0:T(4,128)S(1)}, f32[36,4,256]{2,1,0:T(4,128)S(1)}, u32[]{:S(2)}, u32[]{:S(2)}) collective-permute-start(f32[36,4,256]{2,1,0:T(4,128)S(1)} %get-tuple-element.23), channel_id=1, source_target_pairs={{0,1},{1,2},{2,3},{3,0},{4,5},{5,6},{6,7},{7,4},{8,9},{9,10},{10,1... | collective-permute-start | bytes 442376 | tf_op jit(solution)/shard_map/ppermute | solution.py:24
  4.8 13.4 %collective-permute-start.2 = (f32[17,8,256]{2,1,0:T(8,128)S(1)}, f32[17,8,256]{2,1,0:T(8,128)S(1)}, u32[]{:S(2)}, u32[]{:S(2)}) collective-permute-start(f32[17,8,256]{2,1,0:T(8,128)S(1)} %get-tuple-element.25), channel_id=1, source_target_pairs={{0,4},{4,8},{8,12},{12,16},{16,20},{20,24},{24,28},{28,0},{1,5},{5... | collective-permute-start | bytes 417800 | tf_op jit(solution)/shard_map/ppermute | solution.py:24
  4.9 8.7 %collective-permute-start.5 = (f32[33,4,256]{2,1,0:T(4,128)S(1)}, f32[33,4,256]{2,1,0:T(4,128)S(1)}, u32[]{:S(2)}, u32[]{:S(2)}) collective-permute-start(f32[33,4,256]{2,1,0:T(4,128)S(1)} %get-tuple-element.30), channel_id=1, source_target_pairs={{0,1},{1,2},{2,3},{3,0},{4,5},{5,6},{6,7},{7,4},{8,9},{9,10},{10,1... | collective-permute-start | bytes 405512 | tf_op jit(solution)/shard_map/ppermute | solution.py:24
  6.4 11.9 %collective-permute-start.1 = (f32[33,4,256]{2,1,0:T(4,128)S(1)}, f32[33,4,256]{2,1,0:T(4,128)S(1)}, u32[]{:S(2)}, u32[]{:S(2)}) collective-permute-start(f32[33,4,256]{2,1,0:T(4,128)S(1)} %get-tuple-element.24), channel_id=1, source_target_pairs={{0,3},{1,0},{2,1},{3,2},{4,7},{5,4},{6,5},{7,6},{8,11},{9,8},{10,9... | collective-permute-start | bytes 405512 | tf_op jit(solution)/shard_map/ppermute | solution.py:24
  8.7 9.6 %collective-permute-start.3 = (f32[16,8,256]{2,1,0:T(8,128)S(1)}, f32[16,8,256]{2,1,0:T(8,128)S(1)}, u32[]{:S(2)}, u32[]{:S(2)}) collective-permute-start(f32[16,8,256]{2,1,0:T(8,128)S(1)} %get-tuple-element.26), channel_id=1, source_target_pairs={{0,28},{4,0},{8,4},{12,8},{16,12},{20,16},{24,20},{28,24},{1,29},{... | collective-permute-start | bytes 393224 | tf_op jit(solution)/shard_map/ppermute | solution.py:24
  13.6 7.1 %collective-permute-start.4 = (f32[31,4,256]{2,1,0:T(4,128)S(1)}, f32[31,4,256]{2,1,0:T(4,128)S(1)}, u32[]{:S(2)}, u32[]{:S(2)}) collective-permute-start(f32[31,4,256]{2,1,0:T(4,128)S(1)} %get-tuple-element.29), channel_id=1, source_target_pairs={{0,3},{1,0},{2,1},{3,2},{4,7},{5,4},{6,5},{7,6},{8,11},{9,8},{10,9... | collective-permute-start | bytes 380936 | tf_op jit(solution)/shard_map/ppermute | solution.py:24
  18.5 3.0 %collective-permute-start.7 = (f32[17,8,256]{2,1,0:T(8,128)S(1)}, f32[17,8,256]{2,1,0:T(8,128)S(1)}, u32[]{:S(2)}, u32[]{:S(2)}) collective-permute-start(f32[17,8,256]{2,1,0:T(8,128)S(1)} %pad_maximum_fusion.3), channel_id=1, source_target_pairs={{0,28},{4,0},{8,4},{12,8},{16,12},{20,16},{24,20},{28,24},{1,29},{... | collective-permute-start | bytes 417800 | tf_op jit(solution)/shard_map/ppermute | solution.py:24
  19.6 6.0 %collective-permute-start.6 = (f32[18,8,256]{2,1,0:T(8,128)S(1)}, f32[18,8,256]{2,1,0:T(8,128)S(1)}, u32[]{:S(2)}, u32[]{:S(2)}) collective-permute-start(f32[18,8,256]{2,1,0:T(8,128)S(1)} %pad_maximum_fusion.2), channel_id=1, source_target_pairs={{0,4},{4,8},{8,12},{12,16},{16,20},{20,24},{24,28},{28,0},{1,5},{5... | collective-permute-start | bytes 442376 | tf_op jit(solution)/shard_map/ppermute | solution.py:24

commit v2 on v1

--- a/solution.py
+++ b/solution.py
@@ -145,7 +145,10 @@
                         q_ref[n, i, j] = out[by, bz][tile]
         return _
 
-    pairs(first, last, forward, 0)
+    even = first + (last - first) // 2 * 2
+    pairs(first, even, forward, 0)
+    for n in range(even, last):
+        forward(n, 0)
 
 
 def voxel_layers(j, first, last, cells_at, q_ref, f_ref):
@@ -251,8 +254,8 @@
 
 def begin_kernel(
     r_own, lab_own, side_a, side_b, edge_a, edge_b,
-    side_out, t_out, inv_out, d_out,
-    edge_ref, turn_ref,
+    side_out, t_out, next_out, inv_out, d_out, sums_out,
+    edge_ref, turn_ref, image_ref, q_ref, f_ref,
 ):
     own_x, own_y, depth = r_own.shape[1:]
 
@@ -272,11 +275,11 @@
     lines = edge_ref[...]
     edge_ref[...] = lines + roll(lines, 1, 1)
     for m in range(own_x):
-        turn_ref[m] = roll(both(lab_own[m], side_out[3, m]), 1, 1)
+        image_ref[0, m] = roll(both(lab_own[m], side_out[3, m]), 1, 1)
 
     def layer(m):
         cells = both(lab_own[m], side_out[3, m])
-        return diagonal_layer(cells, turn_ref[m], edge_ref[pl.ds(m, 1), :], own_y + HALO)
+        return diagonal_layer(cells, image_ref[0, m], edge_ref[pl.ds(m, 1), :], own_y + HALO)
 
     def start(x, before):
         here = layer(x)
@@ -291,9 +294,45 @@
     before = pairs(1, own_x - 1, start, layer(0))
     start(own_x - 1, before)
 
+    forward_planes(1, own_x, t_out, turn_ref, q_ref)
+    for j, (line, lanes) in enumerate(tiles_of(own_y + side_a.shape[1], depth)):
+
+        def cells_at(n):
+            if line.start < own_y:
+                return lab_own[n, line, lanes]
+            return side_out[3, n, line.start - own_y : line.stop - own_y, lanes]
+
+        voxel_layers(j, 1, own_x - 1, cells_at, q_ref, f_ref)
+
+    def advance(x, acc):
+        energy, right = acc
+        new = update(0, inv_out[x])
+        for comp in range(3):
+            t = get(t_out, comp, x)
+            force = image_ref[comp, x]
+            energy += t[:own_y] * (force[:own_y] + KAPPA * t[:own_y])
+            right += t[:own_y] * r_own[comp, x]
+            put(next_out, comp, x, value=new(force, t, None))
+        return energy, right
+
+    def several(n, acc):
+        for u in range(WIDTH):
+            acc = advance(n + u, acc)
+        for u in range(WIDTH):
+            collect(n + WIDTH + u, f_ref, image_ref)
+        return acc
+
+    for x in range(2, 2 + WIDTH):
+        collect(x, f_ref, image_ref)
+    whole = 2 + (own_x - 3) // WIDTH * WIDTH
+    acc = strides(2, whole, WIDTH, several, (jnp.zeros((own_y, depth), jnp.float32),) * 2)
+    for x in range(whole, own_x - 1):
+        acc = advance(x, acc)
+    sums_out[...] = packed_sums(acc)
+
 
 def basis_kernel(
-    r_own, lab_own, side_ref, edge_a, below, above, below_side, above_side, t0_in, inv_in,
+    r_own, lab_own, side_ref, edge_a, below, above, below_side, above_side, t0_in, t1_in, inv_in, sums_in,
     t_out, d_out, sums_out,
     cell_ref, inv_ref, t_ref, turn_ref, image_ref, q_ref, f_ref,
 ):
@@ -333,6 +372,9 @@
             t = get(t0_in, comp, x)
             put(t_ref, 0, comp, x + h, value=t)
             t_out[0, comp, x] = t[:own_y]
+            t = get(t1_in, comp, x)
+            put(t_ref, 1, comp, x + h, value=t)
+            t_out[1, comp, x] = t[:own_y]
         return _
 
     pairs(0, own_x, copy, 0)
@@ -359,9 +401,13 @@
     totals = []
     for k in range(ITERS):
         first, last = k, planes - k
-        forward_planes(first, last, t_ref.at[k], turn_ref, q_ref)
+        runs = [(first, last)] if k > 0 else [(0, h + 3), (planes - h - 2, planes)]
+        for start, stop in runs:
+            forward_planes(start, stop, t_ref.at[k], turn_ref, q_ref)
         for j, (line, lanes) in enumerate(tiles):
-            voxel_layers(j, first, last - 1, lambda n: cell_ref[n + 1, line, lanes], q_ref, f_ref)
+            for start, stop in runs:
+                cells_at = lambda n: cell_ref[n + 1, line, lanes]
+                voxel_layers(j, start, stop - 1, cells_at, q_ref, f_ref)
 
         def advance(n, own, acc):
             acc = list(acc)
@@ -388,6 +434,16 @@
                 collect(n + WIDTH + u, f_ref, image_ref)
             return acc
 
+        if k == 0:
+            ends = [n for start, stop in runs for n in range(start + 1, stop - 1)]
+            for n in ends:
+                collect(n, f_ref, image_ref)
+            acc = (jnp.zeros((own_y, depth), jnp.float32),) * 2
+            for n in ends:
+                acc = advance(n, lo <= n < hi, acc)
+            totals.extend(acc)
+            continue
+
         beside = [*range(first + 1, lo), *range(hi, last - 1)] if k + 1 < ITERS else []
         for n in [*beside, *range(lo, lo + WIDTH)]:
             collect(n, f_ref, image_ref)
@@ -399,7 +455,7 @@
         for n in range(whole, hi):
             acc = advance(n, True, acc)
         totals.extend(acc)
-    sums_out[...] = jnp.broadcast_to(packed_sums(totals)[None], sums_out.shape)
+    sums_out[...] = jnp.broadcast_to((packed_sums(totals) + sums_in[...])[None], sums_out.shape)
 
 
 def pack_kernel(
@@ -563,19 +619,19 @@
             kept(planes, len(MODES)),
         ]
 
-    side, t0, inverse, diagonal = pl.pallas_call(
+    own_kept = jax.ShapeDtypeStruct((3, own_x, across, rows + 8, 128), f32)
+    side, t0, t1, inverse, diagonal, first_sums = pl.pallas_call(
         begin_kernel,
         out_shape=(
             jax.ShapeDtypeStruct((4, own_x, 2 * h, depth), f32),
-            jax.ShapeDtypeStruct((3, own_x, across, rows + 8, 128), f32),
+            own_kept,
+            own_kept,
             jax.ShapeDtypeStruct((own_x, rows, depth), f32),
             jax.ShapeDtypeStruct((own_x, own_y, depth), f32),
+            jax.ShapeDtypeStruct((1, 128), f32),
         ),
-        scratch_shapes=[
-            pltpu.VMEM((own_x, depth), f32),
-            pltpu.VMEM((own_x, rows, depth), f32),
-        ],
-        compiler_params=small,
+        scratch_shapes=[pltpu.VMEM((own_x, depth), f32), *scratch(own_x + WIDTH)[1:]],
+        compiler_params=pltpu.CompilerParams(vmem_limit_bytes=24 * 2**20),
         name="begin",
     )(right_side, lab, side_a, side_b, edge_a, edge_b)
 
@@ -594,7 +650,10 @@
         ],
         compiler_params=pltpu.CompilerParams(vmem_limit_bytes=34 * 2**20),
         name="basis",
-    )(right_side, lab, side, edge_a, below, above, below_side, above_side, t0, inverse)
+    )(
+        right_side, lab, side, edge_a, below, above, below_side, above_side,
+        t0, t1, inverse, first_sums,
+    )
 
     everyone = lax.all_to_all(sums, ("gx", "gy"), 0, 0)
     out = jax.ShapeDtypeStruct(right_side.shape, f32)

time: 48.6 us -> 48.9 us (level)
  blocking collectives: 9.22 us -> 11.3 us
  waiting for transfers between devices: 8.03 us -> 6.54 us
  other arithmetic: 0.92 us -> 0.27 us
    pallas_call x1, Pallas kernels: 0.37 us -> 2.52 us  [local(): pl.pallas_call(begin_kernel, out_shape=(jax.ShapeDtypeStruct((4, own_x, 2...]
    all_to_all x1, blocking collectives: 9.22 us -> 11.3 us  [local(): everyone = lax.all_to_all(sums, ('gx', 'gy'), 0, 0)]
    pallas_call x1, Pallas kernels: 12.3 us -> 10.6 us  [local(): pl.pallas_call(basis_kernel, out_shape=(jax.ShapeDtypeStruct((ITERS + 1,...]
    ppermute x8, waiting for transfers between devices: 8.03 us -> 6.54 us  [shifted(): lax.ppermute(shard, axis, [(i, (i + by) % size) for i in range(size)])]
    pad x1, other arithmetic: 0.73 us -> 0.07 us  [corner(): rows = jnp.pad(rows, ((0, 2 * h - rows.shape[0]), (0, 0)))]
  transfers between devices with their start and end apart: 8 -> 8, of which waited for: 4 -> 3; matrix products, arithmetic and copies ran while one was open for 2% -> 1% of each run, Pallas kernels for 1% -> 5%
where the time goes in v2:
time: 48.9 us; the launch traced here: 48.8 us
  Pallas kernels  15.5 us (32%)
  starting transfers between devices  14.3 us (29%)
  blocking collectives  11.3 us (23%)
  waiting for transfers between devices  6.54 us (13%)
  between operations  0.79 us (2%)
    ppermute x8, starting transfers between devices, shifted(): lax.ppermute(shard, axis, [(i, (i + by) % size) for i in range(size)])  14.3 us
    all_to_all x1, blocking collectives, local(): everyone = lax.all_to_all(sums, ('gx', 'gy'), 0, 0)  11.3 us
    pallas_call x1, Pallas kernels, local(): pl.pallas_call(basis_kernel, out_shape=(jax.ShapeDtypeStruct((ITERS + 1,...  10.6 us
    ppermute x8, waiting for transfers between devices, shifted(): lax.ppermute(shard, axis, [(i, (i + by) % size) for i in range(size)])  6.54 us
    pallas_call x1, Pallas kernels, local(): pl.pallas_call(begin_kernel, out_shape=(jax.ShapeDtypeStruct((4, own_x, 2...  2.52 us
    pallas_call x1, Pallas kernels, local(): pl.pallas_call(combine_kernel, out_shape=(out, out), compiler_params=smal...  1.27 us
    pallas_call x1, Pallas kernels, local(): pl.pallas_call(pack_kernel, out_shape=(jax.ShapeDtypeStruct(right_side.sh...  1.11 us
  transfers between devices with their start and end apart: 8, of which 3 were waited for; matrix products, arithmetic and copies ran while one was open for 1% of the time, Pallas kernels for 5%

profile of v2, /device:TPU:0, one launch (start us, length us, event | category | flops | bytes accessed | tf_op | source)
XLA Modules:
  0.0 48.8 jit_solution(16067334478851016396)
XLA Ops:
  0.6 0.0 copy-start
  0.6 1.1 %pack.1 = (f32[3,16,8,256]{3,2,1,0:T(8,128)S(1)}, f32[16,8,256]{2,1,0:T(8,128)S(1)}, f32[36,4,256]{2,1,0:T(4,128)S(1)}, f32[33,4,256]{2,1,0:T(4,128)S(1)}, f32[3...) custom-call(f32[3,16,8,256]{3,2,1,0:T(8,128)} %r_hbm.1, ...), custom_call_target="tpu_custom_call" | custom-call | tf_op jit(solution)/shard_map/pack/pallas_call | solution.py:567
  1.8 3.1 %collective-permute-start = (f32[36,4,256]{2,1,0:T(4,128)S(1)}, f32[36,4,256]{2,1,0:T(4,128)S(1)}, u32[]{:S(2)}, u32[]{:S(2)}) collective-permute-start(f32[36,4,256]{2,1,0:T(4,128)S(1)} %get-tuple-element.25), channel_id=1, source_target_pairs={{0,1},{1,2},{2,3},{3,0},{4,5},{5,6},{6,7},{7,4},{8,9},{9,10},{10,1... | collective-permute-start | bytes 442376 | tf_op jit(solution)/shard_map/ppermute | solution.py:24
  4.9 0.0 collective-permute-start.2
  4.9 1.6 %collective-permute-start.5 = (f32[33,4,256]{2,1,0:T(4,128)S(1)}, f32[33,4,256]{2,1,0:T(4,128)S(1)}, u32[]{:S(2)}, u32[]{:S(2)}) collective-permute-start(f32[33,4,256]{2,1,0:T(4,128)S(1)} %get-tuple-element.32), channel_id=1, source_target_pairs={{0,1},{1,2},{2,3},{3,0},{4,5},{5,6},{6,7},{7,4},{8,9},{9,10},{10,1... | collective-permute-start | bytes 405512 | tf_op jit(solution)/shard_map/ppermute | solution.py:24
  6.4 2.2 %collective-permute-start.1 = (f32[33,4,256]{2,1,0:T(4,128)S(1)}, f32[33,4,256]{2,1,0:T(4,128)S(1)}, u32[]{:S(2)}, u32[]{:S(2)}) collective-permute-start(f32[33,4,256]{2,1,0:T(4,128)S(1)} %get-tuple-element.26), channel_id=1, source_target_pairs={{0,3},{1,0},{2,1},{3,2},{4,7},{5,4},{6,5},{7,6},{8,11},{9,8},{10,9... | collective-permute-start | bytes 405512 | tf_op jit(solution)/shard_map/ppermute | solution.py:24
  8.7 2.1 %collective-permute-start.3 = (f32[16,8,256]{2,1,0:T(8,128)S(1)}, f32[16,8,256]{2,1,0:T(8,128)S(1)}, u32[]{:S(2)}, u32[]{:S(2)}) collective-permute-start(f32[16,8,256]{2,1,0:T(8,128)S(1)} %get-tuple-element.28), channel_id=1, source_target_pairs={{0,28},{4,0},{8,4},{12,8},{16,12},{20,16},{24,20},{28,24},{1,29},{... | collective-permute-start | bytes 393224 | tf_op jit(solution)/shard_map/ppermute | solution.py:24
  10.8 2.8 %collective-permute-done.5 = f32[33,4,256]{2,1,0:T(4,128)S(1)} collective-permute-done((f32[33,4,256]{2,1,0:T(4,128)S(1)}, f32[33,4,256]{2,1,0:T(4,128)S(1)}, u32[]{:S(2)}, u32[]{:S(2)}) %collective-permute-start.5) | collective-permute-done | bytes 135200 | tf_op jit(solution)/shard_map/ppermute | solution.py:24
  13.6 4.7 %collective-permute-start.4 = (f32[31,4,256]{2,1,0:T(4,128)S(1)}, f32[31,4,256]{2,1,0:T(4,128)S(1)}, u32[]{:S(2)}, u32[]{:S(2)}) collective-permute-start(f32[31,4,256]{2,1,0:T(4,128)S(1)} %get-tuple-element.31), channel_id=1, source_target_pairs={{0,3},{1,0},{2,1},{3,2},{4,7},{5,4},{6,5},{7,6},{8,11},{9,8},{10,9... | collective-permute-start | bytes 380936 | tf_op jit(solution)/shard_map/ppermute | solution.py:24
  18.3 0.0 collective-permute-done.3.above
  18.3 0.0 collective-permute-done.1
  18.3 0.0 collective-permute-done.2.below
  18.3 0.0 collective-permute-done
  18.5 0.4 collective-permute-start.7
  18.8 0.0 copy-done
  18.8 0.1 broadcast_select_fusion
  19.0 0.3 collective-permute-start.6
  19.2 1.5 %collective-permute-done.4 = f32[31,4,256]{2,1,0:T(4,128)S(1)} collective-permute-done((f32[31,4,256]{2,1,0:T(4,128)S(1)}, f32[31,4,256]{2,1,0:T(4,128)S(1)}, u32[]{:S(2)}, u32[]{:S(2)}) %collective-permute-start.4) | collective-permute-done | bytes 127008 | tf_op jit(solution)/shard_map/ppermute | solution.py:24
  20.8 0.1 pad_maximum_fusion.1.side_b
  20.8 0.1 pad_maximum_fusion.side_a
  20.9 2.5 %begin.1 = (f32[4,16,8,256]{3,2,1,0:T(8,128)S(1)}, f32[3,16,2,24,128]{4,3,2,1,0:T(8,128)S(1)}, f32[3,16,2,24,128]{4,3,2,1,0:T(8,128)S(1)}, f32[16,16,256]{2,1,0:...) custom-call(f32[3,16,8,256]{3,2,1,0:T(8,128)S(1)} %get-tuple-element.23.r_own, ...), custom_call_target="tpu_custom_call" | custom-call | tf_op jit(solution)/shard_map/begin/pallas_call | solution.py:623
  23.4 0.0 collective-permute-done.7.above_side
  23.4 2.2 %collective-permute-done.6.below_side = f32[18,8,256]{2,1,0:T(8,128)S(1)} collective-permute-done((f32[18,8,256]{2,1,0:T(8,128)S(1)}, f32[18,8,256]{2,1,0:T(8,128)S(1)}, u32[]{:S(2)}, u32[]{:S(2)}) %collective-permute-start.6) | collective-permute-done | bytes 147488 | tf_op jit(solution)/shard_map/ppermute | solution.py:24
  25.6 10.6 %basis.1 = (f32[5,3,16,8,256]{4,3,2,1,0:T(8,128)S(1)}, f32[8,256]{1,0:T(8,128)S(1)}, f32[32,1,128]{2,1,0:T(1,128)S(1)}) custom-call(f32[3,16,8,256]{3,2,1,0:T(8,128)S(1)} %get-tuple-element.23.r_own, f32[16,8,256]{2,1,0:T(8,128)S(1)} %get-tuple-element.24.lab_own, f32[4,16,8,256]{3,2,1,0:T(8,128)S(1)} %get-tuple-element.33.side_ref, ...), custom_call_target="tpu_custom_call" | custom-call | tf_op jit(solution)/shard_map/basis/pallas_call | solution.py:639
  36.2 11.3 %all_to_all.5 = f32[32,1,128]{2,1,0:T(1,128)S(1)} all-to-all(f32[32,1,128]{2,1,0:T(1,128)S(1)} %get-tuple-element.40), channel_id=1, replica_groups=mesh['gx'=8,'gy'=4] {'gx','gy'}, dimensions={0} | all-to-all | bytes 32768 | tf_op jit(solution)/shard_map/all_to_all | solution.py:658
  47.5 1.3 %combine.1 = (f32[3,16,8,256]{3,2,1,0:T(8,128)}, f32[3,16,8,256]{3,2,1,0:T(8,128)}) custom-call(f32[32,128]{1,0:T(8,128)S(1)} %bitcast.3, f32[5,3,16,8,256]{4,3,2,1,0:T(8,128)S(1)} %get-tuple-element.41.t_ref, f32[16,8,256]{2,1,0:T(8,128)S(1)} %get-tuple-element.42.d_ref, f32[8,256]{1,0:T(8,128)S(1)} %get-tuple-element.43.d_first), custom_call_target="tpu_custom_call" | custom-call | tf_op jit(solution)/shard_map/combine/pallas_call | solution.py:660
  (14 shorter events, 0.2 us)
Async XLA Ops:
  0.6 18.2 %copy-start = (pred[8]{0:T(512)(128)(4,1)S(1)}, pred[8]{0:T(512)(128)(4,1)}, u32[]{:S(2)}) copy-start(pred[8]{0:T(512)(128)(4,1)} %constant.3.clone.1) | copy-start | bytes 28
  1.8 16.6 %collective-permute-start = (f32[36,4,256]{2,1,0:T(4,128)S(1)}, f32[36,4,256]{2,1,0:T(4,128)S(1)}, u32[]{:S(2)}, u32[]{:S(2)}) collective-permute-start(f32[36,4,256]{2,1,0:T(4,128)S(1)} %get-tuple-element.25), channel_id=1, source_target_pairs={{0,1},{1,2},{2,3},{3,0},{4,5},{5,6},{6,7},{7,4},{8,9},{9,10},{10,1... | collective-permute-start | bytes 442376 | tf_op jit(solution)/shard_map/ppermute | solution.py:24
  4.9 13.4 %collective-permute-start.2 = (f32[17,8,256]{2,1,0:T(8,128)S(1)}, f32[17,8,256]{2,1,0:T(8,128)S(1)}, u32[]{:S(2)}, u32[]{:S(2)}) collective-permute-start(f32[17,8,256]{2,1,0:T(8,128)S(1)} %get-tuple-element.27), channel_id=1, source_target_pairs={{0,4},{4,8},{8,12},{12,16},{16,20},{20,24},{24,28},{28,0},{1,5},{5... | collective-permute-start | bytes 417800 | tf_op jit(solution)/shard_map/ppermute | solution.py:24
  4.9 8.7 %collective-permute-start.5 = (f32[33,4,256]{2,1,0:T(4,128)S(1)}, f32[33,4,256]{2,1,0:T(4,128)S(1)}, u32[]{:S(2)}, u32[]{:S(2)}) collective-permute-start(f32[33,4,256]{2,1,0:T(4,128)S(1)} %get-tuple-element.32), channel_id=1, source_target_pairs={{0,1},{1,2},{2,3},{3,0},{4,5},{5,6},{6,7},{7,4},{8,9},{9,10},{10,1... | collective-permute-start | bytes 405512 | tf_op jit(solution)/shard_map/ppermute | solution.py:24
  6.4 11.9 %collective-permute-start.1 = (f32[33,4,256]{2,1,0:T(4,128)S(1)}, f32[33,4,256]{2,1,0:T(4,128)S(1)}, u32[]{:S(2)}, u32[]{:S(2)}) collective-permute-start(f32[33,4,256]{2,1,0:T(4,128)S(1)} %get-tuple-element.26), channel_id=1, source_target_pairs={{0,3},{1,0},{2,1},{3,2},{4,7},{5,4},{6,5},{7,6},{8,11},{9,8},{10,9... | collective-permute-start | bytes 405512 | tf_op jit(solution)/shard_map/ppermute | solution.py:24
  8.7 9.6 %collective-permute-start.3 = (f32[16,8,256]{2,1,0:T(8,128)S(1)}, f32[16,8,256]{2,1,0:T(8,128)S(1)}, u32[]{:S(2)}, u32[]{:S(2)}) collective-permute-start(f32[16,8,256]{2,1,0:T(8,128)S(1)} %get-tuple-element.28), channel_id=1, source_target_pairs={{0,28},{4,0},{8,4},{12,8},{16,12},{20,16},{24,20},{28,24},{1,29},{... | collective-permute-start | bytes 393224 | tf_op jit(solution)/shard_map/ppermute | solution.py:24
  13.6 7.1 %collective-permute-start.4 = (f32[31,4,256]{2,1,0:T(4,128)S(1)}, f32[31,4,256]{2,1,0:T(4,128)S(1)}, u32[]{:S(2)}, u32[]{:S(2)}) collective-permute-start(f32[31,4,256]{2,1,0:T(4,128)S(1)} %get-tuple-element.31), channel_id=1, source_target_pairs={{0,3},{1,0},{2,1},{3,2},{4,7},{5,4},{6,5},{7,6},{8,11},{9,8},{10,9... | collective-permute-start | bytes 380936 | tf_op jit(solution)/shard_map/ppermute | solution.py:24
  18.5 4.9 %collective-permute-start.7 = (f32[17,8,256]{2,1,0:T(8,128)S(1)}, f32[17,8,256]{2,1,0:T(8,128)S(1)}, u32[]{:S(2)}, u32[]{:S(2)}) collective-permute-start(f32[17,8,256]{2,1,0:T(8,128)S(1)} %pad_maximum_fusion.3), channel_id=1, source_target_pairs={{0,28},{4,0},{8,4},{12,8},{16,12},{20,16},{24,20},{28,24},{1,29},{... | collective-permute-start | bytes 417800 | tf_op jit(solution)/shard_map/ppermute | solution.py:24
  19.0 6.6 %collective-permute-start.6 = (f32[18,8,256]{2,1,0:T(8,128)S(1)}, f32[18,8,256]{2,1,0:T(8,128)S(1)}, u32[]{:S(2)}, u32[]{:S(2)}) collective-permute-start(f32[18,8,256]{2,1,0:T(8,128)S(1)} %pad_maximum_fusion.2), channel_id=1, source_target_pairs={{0,4},{4,8},{8,12},{12,16},{16,20},{20,24},{24,28},{28,0},{1,5},{5... | collective-permute-start | bytes 442376 | tf_op jit(solution)/shard_map/ppermute | solution.py:24

commit v3 on v2

--- a/solution.py
+++ b/solution.py
@@ -124,12 +124,14 @@
     return base + ((LAMBDA_RISE + 4 * SHEAR_RISE) / 9) * two_layers
 
 
+def turn_plane(n, node_ref, turn_ref):
+    for comp in range(3):
+        put(turn_ref, comp, n, value=roll(get(node_ref, comp, n), -1, 1))
+
+
 def forward_planes(first, last, node_ref, turn_ref, q_ref):
     rows = node_ref.shape[-2] - 8
     tiles = tiles_of(rows, 128 * node_ref.shape[-3])
-    for n in range(first, last):
-        for comp in range(3):
-            put(turn_ref, comp, n, value=roll(get(node_ref, comp, n), -1, 1))
 
     def forward(n, _):
         for comp in range(3):
@@ -183,11 +185,7 @@
         return far, ahead
 
     near = [q_ref[first, i, j] for i in range(len(MODES))]
-    carry = near, [jnp.zeros_like(v) for v in near]
-    even = first + (last - first) // 2 * 2
-    carry = pairs(first, even, voxels, carry)
-    for n in range(even, last):
-        carry = voxels(n, carry)
+    pairs(first, last, voxels, (near, [jnp.zeros_like(v) for v in near]))
 
 
 def collect(n, f_ref, image_ref):
@@ -254,7 +252,7 @@
 
 def begin_kernel(
     r_own, lab_own, side_a, side_b, edge_a, edge_b,
-    side_out, t_out, next_out, inv_out, d_out, sums_out,
+    side_out, t_out, next_out, next_turn, inv_out, d_out, sums_out,
     edge_ref, turn_ref, image_ref, q_ref, f_ref,
 ):
     own_x, own_y, depth = r_own.shape[1:]
@@ -294,6 +292,8 @@
     before = pairs(1, own_x - 1, start, layer(0))
     start(own_x - 1, before)
 
+    for x in range(1, own_x):
+        turn_plane(x, t_out, turn_ref)
     forward_planes(1, own_x, t_out, turn_ref, q_ref)
     for j, (line, lanes) in enumerate(tiles_of(own_y + side_a.shape[1], depth)):
 
@@ -312,10 +312,12 @@
             force = image_ref[comp, x]
             energy += t[:own_y] * (force[:own_y] + KAPPA * t[:own_y])
             right += t[:own_y] * r_own[comp, x]
-            put(next_out, comp, x, value=new(force, t, None))
+            put(next_out, comp, x + HALO, value=new(force, t, None))
         return energy, right
 
     def several(n, acc):
+        for u in range(WIDTH):
+            turn_plane(n + HALO - WIDTH + u, next_out, next_turn)
         for u in range(WIDTH):
             acc = advance(n + u, acc)
         for u in range(WIDTH):
@@ -328,11 +330,13 @@
     acc = strides(2, whole, WIDTH, several, (jnp.zeros((own_y, depth), jnp.float32),) * 2)
     for x in range(whole, own_x - 1):
         acc = advance(x, acc)
+    for x in range(whole - WIDTH, own_x - 1):
+        turn_plane(x + HALO, next_out, next_turn)
     sums_out[...] = packed_sums(acc)
 
 
 def basis_kernel(
-    r_own, lab_own, side_ref, edge_a, below, above, below_side, above_side, t0_in, t1_in, inv_in, sums_in,
+    r_own, lab_own, side_ref, edge_a, below, above, below_side, above_side, t0_in, t1_in, turn1_in, inv_in, sums_in,
     t_out, d_out, sums_out,
     cell_ref, inv_ref, t_ref, turn_ref, image_ref, q_ref, f_ref,
 ):
@@ -372,7 +376,7 @@
             t = get(t0_in, comp, x)
             put(t_ref, 0, comp, x + h, value=t)
             t_out[0, comp, x] = t[:own_y]
-            t = get(t1_in, comp, x)
+            t = get(t1_in, comp, x + h)
             put(t_ref, 1, comp, x + h, value=t)
             t_out[1, comp, x] = t[:own_y]
         return _
@@ -402,8 +406,19 @@
     for k in range(ITERS):
         first, last = k, planes - k
         runs = [(first, last)] if k > 0 else [(0, h + 3), (planes - h - 2, planes)]
-        for start, stop in runs:
-            forward_planes(start, stop, t_ref.at[k], turn_ref, q_ref)
+        if k == 0:
+            for start, stop in runs:
+                for n in range(start, stop):
+                    turn_plane(n, t_ref.at[k], turn_ref)
+                forward_planes(start, stop, t_ref.at[k], turn_ref, q_ref)
+        elif k == 1:
+            for start, stop in ((first, lo + 2), (hi - 1, last)):
+                for n in range(start, stop):
+                    turn_plane(n, t_ref.at[k], turn_ref)
+                forward_planes(start, stop, t_ref.at[k], turn_ref, q_ref)
+            forward_planes(lo + 2, hi - 1, t1_in, turn1_in, q_ref)
+        else:
+            forward_planes(first, last, t_ref.at[k], turn_ref, q_ref)
         for j, (line, lanes) in enumerate(tiles):
             for start, stop in runs:
                 cells_at = lambda n: cell_ref[n + 1, line, lanes]
@@ -428,6 +443,9 @@
             return tuple(acc)
 
         def several(n, acc):
+            if k + 1 < ITERS:
+                for u in range(WIDTH):
+                    turn_plane(n - WIDTH + u, t_ref.at[k + 1], turn_ref)
             for u in range(WIDTH):
                 acc = advance(n + u, True, acc)
             for u in range(WIDTH):
@@ -454,6 +472,9 @@
         acc = strides(lo, whole, WIDTH, several, acc)
         for n in range(whole, hi):
             acc = advance(n, True, acc)
+        if k + 1 < ITERS:
+            for n in range(whole - WIDTH, last - 1):
+                turn_plane(n, t_ref.at[k + 1], turn_ref)
         totals.extend(acc)
     sums_out[...] = jnp.broadcast_to((packed_sums(totals) + sums_in[...])[None], sums_out.shape)
 
@@ -620,12 +641,14 @@
         ]
 
     own_kept = jax.ShapeDtypeStruct((3, own_x, across, rows + 8, 128), f32)
-    side, t0, t1, inverse, diagonal, first_sums = pl.pallas_call(
+    next_kept = jax.ShapeDtypeStruct((3, own_x + h, across, rows + 8, 128), f32)
+    side, t0, t1, turn1, inverse, diagonal, first_sums = pl.pallas_call(
         begin_kernel,
         out_shape=(
             jax.ShapeDtypeStruct((4, own_x, 2 * h, depth), f32),
             own_kept,
-            own_kept,
+            next_kept,
+            next_kept,
             jax.ShapeDtypeStruct((own_x, rows, depth), f32),
             jax.ShapeDtypeStruct((own_x, own_y, depth), f32),
             jax.ShapeDtypeStruct((1, 128), f32),
@@ -652,7 +675,7 @@
         name="basis",
     )(
         right_side, lab, side, edge_a, below, above, below_side, above_side,
-        t0, t1, inverse, first_sums,
+        t0, t1, turn1, inverse, first_sums,
     )
 
     everyone = lax.all_to_all(sums, ("gx", "gy"), 0, 0)

time: 48.9 us -> 49.3 us (level)
  transfers between devices with their start and end apart: 8 -> 8, of which waited for: 3 -> 3; matrix products, arithmetic and copies ran while one was open for 1% -> 1% of each run, Pallas kernels for 5% -> 6%
where the time goes in v3:
time: 49.3 us; the launch traced here: 49.1 us
  Pallas kernels  15.8 us (32%)
  starting transfers between devices  14.3 us (29%)
  blocking collectives  11.6 us (24%)
  waiting for transfers between devices  6.34 us (13%)
  between operations  0.8 us (2%)
    ppermute x8, starting transfers between devices, shifted(): lax.ppermute(shard, axis, [(i, (i + by) % size) for i in range(size)])  14.3 us
    all_to_all x1, blocking collectives, local(): everyone = lax.all_to_all(sums, ('gx', 'gy'), 0, 0)  11.6 us
    pallas_call x1, Pallas kernels, local(): pl.pallas_call(basis_kernel, out_shape=(jax.ShapeDtypeStruct((ITERS + 1,...  10.7 us
    ppermute x8, waiting for transfers between devices, shifted(): lax.ppermute(shard, axis, [(i, (i + by) % size) for i in range(size)])  6.34 us
    pallas_call x1, Pallas kernels, local(): pl.pallas_call(begin_kernel, out_shape=(jax.ShapeDtypeStruct((4, own_x, 2...  2.71 us
    pallas_call x1, Pallas kernels, local(): pl.pallas_call(combine_kernel, out_shape=(out, out), compiler_params=smal...  1.27 us
    pallas_call x1, Pallas kernels, local(): pl.pallas_call(pack_kernel, out_shape=(jax.ShapeDtypeStruct(right_side.sh...  1.11 us
  transfers between devices with their start and end apart: 8, of which 3 were waited for; matrix products, arithmetic and copies ran while one was open for 1% of the time, Pallas kernels for 6%

profile of v3, /device:TPU:0, one launch (start us, length us, event | category | flops | bytes accessed | tf_op | source)
XLA Modules:
  0.0 49.1 jit_solution(13056521926652967636)
XLA Ops:
  0.6 0.0 copy-start
  0.6 1.1 %pack.1 = (f32[3,16,8,256]{3,2,1,0:T(8,128)S(1)}, f32[16,8,256]{2,1,0:T(8,128)S(1)}, f32[36,4,256]{2,1,0:T(4,128)S(1)}, f32[33,4,256]{2,1,0:T(4,128)S(1)}, f32[3...) custom-call(f32[3,16,8,256]{3,2,1,0:T(8,128)} %r_hbm.1, ...), custom_call_target="tpu_custom_call" | custom-call | tf_op jit(solution)/shard_map/pack/pallas_call | solution.py:588
  1.8 3.1 %collective-permute-start = (f32[36,4,256]{2,1,0:T(4,128)S(1)}, f32[36,4,256]{2,1,0:T(4,128)S(1)}, u32[]{:S(2)}, u32[]{:S(2)}) collective-permute-start(f32[36,4,256]{2,1,0:T(4,128)S(1)} %get-tuple-element.26), channel_id=1, source_target_pairs={{0,1},{1,2},{2,3},{3,0},{4,5},{5,6},{6,7},{7,4},{8,9},{9,10},{10,1... | collective-permute-start | bytes 442376 | tf_op jit(solution)/shard_map/ppermute | solution.py:24
  4.9 0.0 collective-permute-start.2
  4.9 1.6 %collective-permute-start.5 = (f32[33,4,256]{2,1,0:T(4,128)S(1)}, f32[33,4,256]{2,1,0:T(4,128)S(1)}, u32[]{:S(2)}, u32[]{:S(2)}) collective-permute-start(f32[33,4,256]{2,1,0:T(4,128)S(1)} %get-tuple-element.33), channel_id=1, source_target_pairs={{0,1},{1,2},{2,3},{3,0},{4,5},{5,6},{6,7},{7,4},{8,9},{9,10},{10,1... | collective-permute-start | bytes 405512 | tf_op jit(solution)/shard_map/ppermute | solution.py:24
  6.4 2.2 %collective-permute-start.1 = (f32[33,4,256]{2,1,0:T(4,128)S(1)}, f32[33,4,256]{2,1,0:T(4,128)S(1)}, u32[]{:S(2)}, u32[]{:S(2)}) collective-permute-start(f32[33,4,256]{2,1,0:T(4,128)S(1)} %get-tuple-element.27), channel_id=1, source_target_pairs={{0,3},{1,0},{2,1},{3,2},{4,7},{5,4},{6,5},{7,6},{8,11},{9,8},{10,9... | collective-permute-start | bytes 405512 | tf_op jit(solution)/shard_map/ppermute | solution.py:24
  8.7 2.1 %collective-permute-start.3 = (f32[16,8,256]{2,1,0:T(8,128)S(1)}, f32[16,8,256]{2,1,0:T(8,128)S(1)}, u32[]{:S(2)}, u32[]{:S(2)}) collective-permute-start(f32[16,8,256]{2,1,0:T(8,128)S(1)} %get-tuple-element.29), channel_id=1, source_target_pairs={{0,28},{4,0},{8,4},{12,8},{16,12},{20,16},{24,20},{28,24},{1,29},{... | collective-permute-start | bytes 393224 | tf_op jit(solution)/shard_map/ppermute | solution.py:24
  10.8 2.8 %collective-permute-done.5 = f32[33,4,256]{2,1,0:T(4,128)S(1)} collective-permute-done((f32[33,4,256]{2,1,0:T(4,128)S(1)}, f32[33,4,256]{2,1,0:T(4,128)S(1)}, u32[]{:S(2)}, u32[]{:S(2)}) %collective-permute-start.5) | collective-permute-done | bytes 135200 | tf_op jit(solution)/shard_map/ppermute | solution.py:24
  13.6 4.7 %collective-permute-start.4 = (f32[31,4,256]{2,1,0:T(4,128)S(1)}, f32[31,4,256]{2,1,0:T(4,128)S(1)}, u32[]{:S(2)}, u32[]{:S(2)}) collective-permute-start(f32[31,4,256]{2,1,0:T(4,128)S(1)} %get-tuple-element.32), channel_id=1, source_target_pairs={{0,3},{1,0},{2,1},{3,2},{4,7},{5,4},{6,5},{7,6},{8,11},{9,8},{10,9... | collective-permute-start | bytes 380936 | tf_op jit(solution)/shard_map/ppermute | solution.py:24
  18.3 0.0 collective-permute-done.3.above
  18.3 0.0 collective-permute-done.1
  18.3 0.0 collective-permute-done.2.below
  18.3 0.0 collective-permute-done
  18.5 0.4 collective-permute-start.7
  18.8 0.0 copy-done
  18.8 0.1 broadcast_select_fusion
  19.0 0.3 collective-permute-start.6
  19.2 1.5 %collective-permute-done.4 = f32[31,4,256]{2,1,0:T(4,128)S(1)} collective-permute-done((f32[31,4,256]{2,1,0:T(4,128)S(1)}, f32[31,4,256]{2,1,0:T(4,128)S(1)}, u32[]{:S(2)}, u32[]{:S(2)}) %collective-permute-start.4) | collective-permute-done | bytes 127008 | tf_op jit(solution)/shard_map/ppermute | solution.py:24
  20.8 0.1 pad_maximum_fusion.1.side_b
  20.8 0.1 pad_maximum_fusion.side_a
  20.9 2.7 %begin.1 = (f32[4,16,8,256]{3,2,1,0:T(8,128)S(1)}, f32[3,16,2,24,128]{4,3,2,1,0:T(8,128)S(1)}, f32[3,20,2,24,128]{4,3,2,1,0:T(8,128)S(1)}, f32[3,20,2,24,128]{4,...) custom-call(f32[3,16,8,256]{3,2,1,0:T(8,128)S(1)} %get-tuple-element.24.r_own, ...), custom_call_target="tpu_custom_call" | custom-call | tf_op jit(solution)/shard_map/begin/pallas_call | solution.py:645
  23.6 0.0 collective-permute-done.7.above_side
  23.6 2.0 %collective-permute-done.6.below_side = f32[18,8,256]{2,1,0:T(8,128)S(1)} collective-permute-done((f32[18,8,256]{2,1,0:T(8,128)S(1)}, f32[18,8,256]{2,1,0:T(8,128)S(1)}, u32[]{:S(2)}, u32[]{:S(2)}) %collective-permute-start.6) | collective-permute-done | bytes 147488 | tf_op jit(solution)/shard_map/ppermute | solution.py:24
  25.6 10.7 %basis.1 = (f32[5,3,16,8,256]{4,3,2,1,0:T(8,128)S(1)}, f32[8,256]{1,0:T(8,128)S(1)}, f32[32,1,128]{2,1,0:T(1,128)S(1)}) custom-call(f32[3,16,8,256]{3,2,1,0:T(8,128)S(1)} %get-tuple-element.24.r_own, f32[16,8,256]{2,1,0:T(8,128)S(1)} %get-tuple-element.25.lab_own, f32[4,16,8,256]{3,2,1,0:T(8,128)S(1)} %get-tuple-element.34.side_ref, ...), custom_call_target="tpu_custom_call" | custom-call | tf_op jit(solution)/shard_map/basis/pallas_call | solution.py:662
  36.3 11.6 %all_to_all.5 = f32[32,1,128]{2,1,0:T(1,128)S(1)} all-to-all(f32[32,1,128]{2,1,0:T(1,128)S(1)} %get-tuple-element.42), channel_id=1, replica_groups=mesh['gx'=8,'gy'=4] {'gx','gy'}, dimensions={0} | all-to-all | bytes 32768 | tf_op jit(solution)/shard_map/all_to_all | solution.py:681
  47.8 1.3 %combine.1 = (f32[3,16,8,256]{3,2,1,0:T(8,128)}, f32[3,16,8,256]{3,2,1,0:T(8,128)}) custom-call(f32[32,128]{1,0:T(8,128)S(1)} %bitcast.3, f32[5,3,16,8,256]{4,3,2,1,0:T(8,128)S(1)} %get-tuple-element.43.t_ref, f32[16,8,256]{2,1,0:T(8,128)S(1)} %get-tuple-element.44.d_ref, f32[8,256]{1,0:T(8,128)S(1)} %get-tuple-element.45.d_first), custom_call_target="tpu_custom_call" | custom-call | tf_op jit(solution)/shard_map/combine/pallas_call | solution.py:683
  (14 shorter events, 0.2 us)
Async XLA Ops:
  0.6 18.2 %copy-start = (pred[8]{0:T(512)(128)(4,1)S(1)}, pred[8]{0:T(512)(128)(4,1)}, u32[]{:S(2)}) copy-start(pred[8]{0:T(512)(128)(4,1)} %constant.3.clone.1) | copy-start | bytes 28
  1.8 16.6 %collective-permute-start = (f32[36,4,256]{2,1,0:T(4,128)S(1)}, f32[36,4,256]{2,1,0:T(4,128)S(1)}, u32[]{:S(2)}, u32[]{:S(2)}) collective-permute-start(f32[36,4,256]{2,1,0:T(4,128)S(1)} %get-tuple-element.26), channel_id=1, source_target_pairs={{0,1},{1,2},{2,3},{3,0},{4,5},{5,6},{6,7},{7,4},{8,9},{9,10},{10,1... | collective-permute-start | bytes 442376 | tf_op jit(solution)/shard_map/ppermute | solution.py:24
  4.9 13.4 %collective-permute-start.2 = (f32[17,8,256]{2,1,0:T(8,128)S(1)}, f32[17,8,256]{2,1,0:T(8,128)S(1)}, u32[]{:S(2)}, u32[]{:S(2)}) collective-permute-start(f32[17,8,256]{2,1,0:T(8,128)S(1)} %get-tuple-element.28), channel_id=1, source_target_pairs={{0,4},{4,8},{8,12},{12,16},{16,20},{20,24},{24,28},{28,0},{1,5},{5... | collective-permute-start | bytes 417800 | tf_op jit(solution)/shard_map/ppermute | solution.py:24
  4.9 8.7 %collective-permute-start.5 = (f32[33,4,256]{2,1,0:T(4,128)S(1)}, f32[33,4,256]{2,1,0:T(4,128)S(1)}, u32[]{:S(2)}, u32[]{:S(2)}) collective-permute-start(f32[33,4,256]{2,1,0:T(4,128)S(1)} %get-tuple-element.33), channel_id=1, source_target_pairs={{0,1},{1,2},{2,3},{3,0},{4,5},{5,6},{6,7},{7,4},{8,9},{9,10},{10,1... | collective-permute-start | bytes 405512 | tf_op jit(solution)/shard_map/ppermute | solution.py:24
  6.4 11.9 %collective-permute-start.1 = (f32[33,4,256]{2,1,0:T(4,128)S(1)}, f32[33,4,256]{2,1,0:T(4,128)S(1)}, u32[]{:S(2)}, u32[]{:S(2)}) collective-permute-start(f32[33,4,256]{2,1,0:T(4,128)S(1)} %get-tuple-element.27), channel_id=1, source_target_pairs={{0,3},{1,0},{2,1},{3,2},{4,7},{5,4},{6,5},{7,6},{8,11},{9,8},{10,9... | collective-permute-start | bytes 405512 | tf_op jit(solution)/shard_map/ppermute | solution.py:24
  8.7 9.6 %collective-permute-start.3 = (f32[16,8,256]{2,1,0:T(8,128)S(1)}, f32[16,8,256]{2,1,0:T(8,128)S(1)}, u32[]{:S(2)}, u32[]{:S(2)}) collective-permute-start(f32[16,8,256]{2,1,0:T(8,128)S(1)} %get-tuple-element.29), channel_id=1, source_target_pairs={{0,28},{4,0},{8,4},{12,8},{16,12},{20,16},{24,20},{28,24},{1,29},{... | collective-permute-start | bytes 393224 | tf_op jit(solution)/shard_map/ppermute | solution.py:24
  13.6 7.1 %collective-permute-start.4 = (f32[31,4,256]{2,1,0:T(4,128)S(1)}, f32[31,4,256]{2,1,0:T(4,128)S(1)}, u32[]{:S(2)}, u32[]{:S(2)}) collective-permute-start(f32[31,4,256]{2,1,0:T(4,128)S(1)} %get-tuple-element.32), channel_id=1, source_target_pairs={{0,3},{1,0},{2,1},{3,2},{4,7},{5,4},{6,5},{7,6},{8,11},{9,8},{10,9... | collective-permute-start | bytes 380936 | tf_op jit(solution)/shard_map/ppermute | solution.py:24
  18.5 5.1 %collective-permute-start.7 = (f32[17,8,256]{2,1,0:T(8,128)S(1)}, f32[17,8,256]{2,1,0:T(8,128)S(1)}, u32[]{:S(2)}, u32[]{:S(2)}) collective-permute-start(f32[17,8,256]{2,1,0:T(8,128)S(1)} %pad_maximum_fusion.3), channel_id=1, source_target_pairs={{0,28},{4,0},{8,4},{12,8},{16,12},{20,16},{24,20},{28,24},{1,29},{... | collective-permute-start | bytes 417800 | tf_op jit(solution)/shard_map/ppermute | solution.py:24
  19.0 6.6 %collective-permute-start.6 = (f32[18,8,256]{2,1,0:T(8,128)S(1)}, f32[18,8,256]{2,1,0:T(8,128)S(1)}, u32[]{:S(2)}, u32[]{:S(2)}) collective-permute-start(f32[18,8,256]{2,1,0:T(8,128)S(1)} %pad_maximum_fusion.2), channel_id=1, source_target_pairs={{0,4},{4,8},{8,12},{12,16},{16,20},{20,24},{24,28},{28,0},{1,5},{5... | collective-permute-start | bytes 442376 | tf_op jit(solution)/shard_map/ppermute | solution.py:24
